TPU v7x, 128 devices: a whole 4x4x4 slice. The times are simulated.
128 devices in a mesh: tp: 4 (over x), dp: 32 (over z, y, core).
Axes of the slice: x: 4, y: 4, z: 4, core: 2. Of those that a mesh axis runs over, the one named last changes fastest.
Arguments:
- hidden: bfloat16 [32, 256, 2560], P('dp')
- residual: float32 [32, 256, 2560], P('dp')
- targets: int32 [32, 256], P('dp')
- embedding: bfloat16 [50288, 2560], P('tp')
- norm_w: float32 [2560], replicated
Outputs:
- output 1: float32 [], replicated
- output 2: float32 [32, 256, 2560], P('dp')
- output 3: float32 [50288, 2560], P('tp')
- output 4: float32 [2560], replicated
All inputs are finite; a program needn't handle non-finite values.
Results may differ from a plain program's by a relative error of at most 0.001.
Values sent between devices are 32-bit elements.
A program may use at most 1 GiB of HBM per device.

v0:
```python
import functools

import jax
import jax.numpy as jnp
from jax import lax
from jax.experimental import pallas as pl
from jax.experimental.pallas import tpu as pltpu
from jax.sharding import PartitionSpec as P


NORM_EPS = 1e-5
LANES = 128
VMEM_LIMIT = 60 * 1024 * 1024
NT = (((1,), (1,)), ((), ()))
SHARE_ROWS = 24
PIECES = (('share', 0, 24), ('direct', 96, 40), ('direct', 136, 40), ('direct', 176, 40), ('direct', 216, 40), ('stats', 256, 8))
PLAN = ((('start', 0), ('start', 1)), (), (), (('start', 2), ('r', 0, 1)), (), (), (('r', 1, 1),), (), (), (), (('r', 2, 1),),
 (('start', 5),), (('x', 1), ('r', 0, 2)), (), (), (), (), (('r', 1, 2), ('f', 1)), (), (),
 (('r', 2, 2), ('r', 5, 1), ('r', 0, 3), ('r', 1, 3), ('x', 2), ('start', 3), ('r', 2, 3), ('r', 5, 2), ('r', 0, 4),
  ('r', 1, 4), ('start', 4), ('r', 3, 1), ('x', 3), ('r', 2, 4), ('r', 5, 3), ('r', 4, 1), ('f', 2), ('x', 4),
  ('r', 3, 2), ('r', 5, 4), ('f', 3), ('f', 4), ('r', 4, 2), ('r', 3, 3), ('r', 4, 3), ('r', 3, 4), ('r', 4, 4)))
VOCAB_BLOCK = 1280
GRAD_CHUNKS = (256, 64)
ROW_BLOCK = 512
TOKEN_BLOCK = 1024
OWN_BLOCKS = 2


RING = 4
HOPS = {1: ((1, 0), (-1, 0), (0, 1), (0, -1)),
        2: ((2, 0), (0, 2), (1, 1), (1, -1), (-1, 1), (-1, -1)),
        3: ((1, 2), (-1, 2), (2, 1), (2, -1)),
        4: ((2, 2),)}


class Exchange:
    def __init__(self, own_ref, stats_ref, all_ref, sems, share_rows):
        self.own_ref, self.stats_ref, self.all_ref = own_ref, stats_ref, all_ref
        self.sems = sems
        self.n_rows = own_ref.shape[0]
        self.share_rows = share_rows
        width = own_ref.shape[1]
        self.quarter, self.half, self.width = width // 4, width // 2, width
        self.x = lax.axis_index('tp')
        dp = lax.axis_index('dp')
        self.core = lax.rem(dp, 2)
        self.y = lax.rem(dp // 2, RING)
        self.z = dp // (2 * RING)

    def at(self, dx=0, dy=0, dz=0, other=False):
        x = lax.rem(self.x + dx + RING, RING)
        y = lax.rem(self.y + dy + RING, RING)
        z = lax.rem(self.z + dz + RING, RING)
        core = 1 - self.core if other else self.core
        return (x, (z * RING + y) * 2 + core)

    def pos(self, hop):
        return lax.rem(self.z + hop[1] + RING, RING) * RING + lax.rem(self.y + hop[0] + RING, RING)

    def rows(self, piece):
        kind, start, size = piece
        if kind == 'share':
            start = pl.multiple_of(self.x * self.share_rows, 8)
        return pl.ds(start, size)

    def block(self, hop, rows, first=0, size=None):
        return self.all_ref.at[self.core, self.pos(hop), rows, pl.ds(first, size or self.width)]

    def send(self, src, dst, device, send, recv):
        pltpu.make_async_remote_copy(
            src_ref=src, dst_ref=dst, send_sem=self.sems[send], recv_sem=recv,
            device_id=device, device_id_type=pl.DeviceIdType.MESH).start()

    def barrier(self):
        sem = pltpu.get_barrier_semaphore()
        peers = [self.at(dx=1), self.at(dx=-1), self.at(dx=2), self.at(dy=1), self.at(dy=-1),
                 self.at(dz=1), self.at(dz=-1), self.at(other=True)]
        for peer in peers:
            pl.semaphore_signal(sem, inc=1, device_id=peer, device_id_type=pl.DeviceIdType.MESH)
        pl.semaphore_wait(sem, len(peers))

    def to_pair(self, src, dst):
        self.send(src, dst, self.at(other=True), 'pair_send', self.sems['pair_recv'])

    def start_own(self):
        dst = self.all_ref.at[self.core, self.pos((0, 0)), pl.ds(0, self.n_rows)]
        pltpu.make_async_copy(self.own_ref, dst, self.sems['local']).start()
        self.to_pair(self.own_ref, dst)

    def start_stats(self):
        dst = self.all_ref.at[self.core, self.pos((0, 0)), pl.ds(self.n_rows, 8)]
        pltpu.make_async_copy(self.stats_ref, dst, self.sems['local']).start()
        self.to_pair(self.stats_ref, dst)

    def plane(self, hop_src, rows, first, size, dy, dz, recv):
        ref = self.block(hop_src, rows, first, size)
        self.send(ref, ref, self.at(dy=dy, dz=dz), 'plane_send', recv)

    def round(self, p, piece, k):
        rows, recv = self.rows(piece), self.sems['plane_recv'].at[p, k - 1]
        q, h = self.quarter, self.half
        if k == 1:
            src = self.stats_ref if piece[0] == 'stats' else self.own_ref.at[rows]
            for dy, dz in HOPS[1]:
                self.send(src, self.block((0, 0), rows), self.at(dy=dy, dz=dz), 'plane_send', recv)
        elif k == 2:
            for s in (1, -1):
                for o in (1, -1):
                    self.plane((o, 0), rows, 0, h, 0, s, recv)
                    self.plane((0, o), rows, h, h, s, 0, recv)
            self.plane((-1, 0), rows, q, h, 1, 0, recv)
            self.plane((0, -1), rows, q, h, 0, 1, recv)
            for first in (0, 3 * q):
                self.plane((1, 0), rows, first, q, -1, 0, recv)
                self.plane((0, 1), rows, first, q, 0, -1, recv)
        elif k == 3:
            for s in (1, -1):
                self.plane((2, 0), rows, 0, h, 0, s, recv)
                self.plane((0, 2), rows, h, h, s, 0, recv)
            for o in (1, -1):
                self.plane((o, -1), rows, q, q, 0, 1, recv)
                self.plane((o, 1), rows, 0, q, 0, -1, recv)
                self.plane((-1, o), rows, h, q, 1, 0, recv)
                self.plane((1, o), rows, 3 * q, q, -1, 0, recv)
        else:
            self.plane((2, -1), rows, q, q, 0, 1, recv)
            self.plane((2, 1), rows, 0, q, 0, -1, recv)
            self.plane((-1, 2), rows, h, q, 1, 0, recv)
            self.plane((1, 2), rows, 3 * q, q, -1, 0, recv)

    def wait(self, ref, sem):
        pltpu.make_async_copy(ref, ref, sem).wait()

    def finish_round(self, p, piece, k):
        n, rows = len(HOPS[k]), self.rows(piece)
        self.wait(self.all_ref.at[0, pl.ds(0, n), pl.ds(0, piece[2])], self.sems['plane_recv'].at[p, k - 1])
        for hop in HOPS[k]:
            ref = self.block(hop, rows)
            self.to_pair(ref, ref)
            if piece[0] == 'share':
                for s in (1, -1):
                    self.send(ref, ref, self.at(dx=s), 'x_send', self.sems['x_recv'].at[k - 1])

    def share_of(self, dx):
        x = lax.rem(self.x + dx + RING, RING)
        return pl.ds(pl.multiple_of(x * self.share_rows, 8), self.share_rows)

    def along_x(self, k):
        n = len(HOPS[k])
        self.wait(self.all_ref.at[0, pl.ds(0, n), pl.ds(0, 2 * self.share_rows)], self.sems['x_recv'].at[k - 1])
        for hop in HOPS[k]:
            for dx, first in ((-1, 0), (1, self.half)):
                rows = self.share_of(dx)
                ref = self.block(hop, rows, first, self.half)
                self.send(ref, ref, self.at(dx=-dx), 'x_send', self.sems['far_recv'].at[k - 1])
                ref = self.block(hop, rows)
                self.to_pair(ref, ref)

    def finish_x(self, k):
        n, rows = len(HOPS[k]), self.share_of(2)
        self.wait(self.all_ref.at[0, pl.ds(0, n), pl.ds(0, self.share_rows)], self.sems['far_recv'].at[k - 1])
        for hop in HOPS[k]:
            ref = self.block(hop, rows)
            self.to_pair(ref, ref)

    def finish(self, pieces):
        n_other = RING * RING - 1
        total = sum(size for _, _, size in pieces)
        self.wait(self.all_ref.at[0], self.sems['pair_recv'])
        self.wait(self.all_ref.at[0], self.sems['pair_send'])
        self.wait(self.all_ref.at[0, pl.ds(0, n_other), pl.ds(0, total)], self.sems['plane_send'])
        self.wait(self.all_ref.at[0, pl.ds(0, n_other), pl.ds(0, 3 * self.share_rows)], self.sems['x_send'])
        self.wait(self.all_ref.at[0, 0], self.sems['local'])


def exchange_kernel(plan, pieces, share_rows, vocab, inv_n, h_ref, own_ref, emb_ref, ids_ref, tgt_ref,
                    all_ref, grad_ref, stats_out_ref, logits_ref, m_ref, s_ref, t_ref, col_ref, stats_ref, part_ref,
                    plane_recv, x_recv, far_recv, pair_recv, plane_send, x_send, pair_send, local, part_recv, part_send):
    step = pl.program_id(0)
    n_tiles, rows, width = logits_ref.shape
    sems = dict(plane_recv=plane_recv, x_recv=x_recv, far_recv=far_recv, pair_recv=pair_recv, plane_send=plane_send,
                x_send=x_send, pair_send=pair_send, local=local)
    ex = Exchange(own_ref, stats_ref, all_ref, sems, share_rows)

    def run(event):
        if event[0] == 'start':
            ex.round(event[1], pieces[event[1]], 1)
        elif event[0] == 'r':
            _, p, k = event
            ex.finish_round(p, pieces[p], k)
            if k < 4:
                ex.round(p, pieces[p], k + 1)
        elif event[0] == 'x':
            ex.along_x(event[1])
        else:
            ex.finish_x(event[1])

    for i, events in enumerate(plan):
        if events:
            @pl.when(step == i)
            def _(i=i, events=events):
                if i == 0:
                    ex.barrier()
                    ex.start_own()
                for event in events:
                    run(event)
                if i == len(plan) - 1:
                    ex.finish(pieces)

    @pl.when(step == 0)
    def _():
        m_ref[...] = jnp.full_like(m_ref, -jnp.inf)
        s_ref[...] = jnp.zeros_like(s_ref)
        t_ref[...] = jnp.zeros_like(t_ref)
        grad_ref[...] = jnp.zeros_like(grad_ref)

    @pl.when(step < n_tiles)
    def _():
        logits = lax.dot_general(h_ref[...], emb_ref[...], NT, preferred_element_type=jnp.float32)
        logits_ref[step] = logits
        lane = lax.broadcasted_iota(jnp.int32, (rows, LANES), 1)
        tgt_sum = t_ref[...]
        parts = []
        for j in range(width // LANES):
            ids = lane + (step * width + j * LANES)
            part = jnp.where(ids < vocab, logits[:, j * LANES:(j + 1) * LANES], -jnp.inf)
            tgt_sum += jnp.where(ids == ids_ref[...], part, 0.0)
            parts.append(part)
        t_ref[...] = tgt_sum
        m_old = m_ref[...]
        m_new = functools.reduce(jnp.maximum, parts, m_old)
        floor = jnp.where(m_new == -jnp.inf, 0.0, m_new)
        s_new = s_ref[...] * jnp.exp(m_old - floor)
        for part in parts:
            s_new += jnp.exp(part - floor)
        m_ref[...] = m_new
        s_ref[...] = s_new

    @pl.when(step == n_tiles)
    def _():
        m_col = jnp.max(m_ref[...], axis=1, keepdims=True)
        s_col = jnp.sum(s_ref[...] * jnp.exp(m_ref[...] - m_col), axis=1, keepdims=True)
        t_col = jnp.sum(t_ref[...], axis=1, keepdims=True)
        lane = lax.broadcasted_iota(jnp.int32, (rows, LANES), 1)
        cols = jnp.where(lane == 0, m_col, jnp.where(lane == 1, s_col, jnp.where(lane == 2, t_col, 0.0)))
        part_ref[ex.x] = cols.T[:8]
        for dx in (1, 2, 3):
            dst = part_ref.at[ex.x]
            pltpu.make_async_remote_copy(
                src_ref=dst, dst_ref=dst, send_sem=part_send, recv_sem=part_recv,
                device_id=ex.at(dx=dx), device_id_type=pl.DeviceIdType.MESH).start()
        ex.wait(part_ref.at[pl.ds(0, 3)], part_recv)
        ex.wait(part_ref.at[pl.ds(0, 3)], part_send)
        m_row = functools.reduce(jnp.maximum, [part_ref[i, 0:1] for i in range(RING)])
        s_row = sum(part_ref[i, 1:2] * jnp.exp(part_ref[i, 0:1] - m_row) for i in range(RING))
        t_row = sum(part_ref[i, 2:3] for i in range(RING))
        sub = lax.broadcasted_iota(jnp.int32, (8, rows), 0)
        values = (m_row, inv_n / s_row, tgt_ref[...], s_row, t_row)
        final = jnp.zeros((8, rows), jnp.float32)
        for i, value in enumerate(values):
            final = jnp.where(sub == i, value, final)
        stats_out_ref[...] = final
        stats_ref[...] = jnp.zeros_like(stats_ref)
        stats_ref[:, :rows] = final
        col_ref[...] = jnp.concatenate([final, jnp.zeros((LANES - 8, rows), jnp.float32)]).T
        ex.start_stats()

    def add_grad(masked):
        tile = step - n_tiles
        ids = lax.broadcasted_iota(jnp.int32, (rows, width), 1) + tile * width
        grad = jnp.exp(logits_ref[tile] - col_ref[:, 0:1]) * col_ref[:, 1:2]
        grad -= jnp.where(ids == ids_ref[...], inv_n, 0.0)
        emb = emb_ref[...]
        if masked:
            grad = jnp.where(ids < vocab, grad, 0.0)
            emb_ids = lax.broadcasted_iota(jnp.int32, emb.shape, 0) + tile * width
            emb = jnp.where(emb_ids < vocab, emb.astype(jnp.float32), 0.0).astype(emb.dtype)
        grad_ref[...] += jnp.dot(grad.astype(jnp.bfloat16), emb, preferred_element_type=jnp.float32)

    pl.when(jnp.logical_and(step >= n_tiles, step < 2 * n_tiles - 1))(lambda: add_grad(False))
    pl.when(step == 2 * n_tiles - 1)(lambda: add_grad(True))


def exchange_tokens(h_act, h_wide, emb, local_ids, tgt_row, inv_n, n_dp):
    rows, width = h_act.shape
    vocab = emb.shape[0]
    n_tiles = pl.cdiv(vocab, VOCAB_BLOCK)
    n_steps = 2 * n_tiles + 1
    plan = PLAN if len(PLAN) == n_steps else PLAN[:-1] + ((),) * (n_steps - len(PLAN)) + PLAN[-1:]
    dma = pltpu.SemaphoreType.DMA
    emb_tile = lambda i: (jnp.where(i < n_tiles, i, jnp.minimum(i - n_tiles, n_tiles - 1)), 0)
    whole = pl.BlockSpec(memory_space=pltpu.VMEM)
    return pl.pallas_call(
        functools.partial(exchange_kernel, plan, PIECES, SHARE_ROWS, vocab, inv_n),
        out_shape=(jax.ShapeDtypeStruct((2, n_dp // 2, rows + 8, width), jnp.float32),
                   jax.ShapeDtypeStruct((rows, width), jnp.float32),
                   jax.ShapeDtypeStruct((8, rows), jnp.float32)),
        grid=(n_steps,),
        in_specs=[whole, whole, pl.BlockSpec((VOCAB_BLOCK, width), emb_tile), whole, whole],
        out_specs=(pl.BlockSpec(memory_space=pl.ANY), whole, whole),
        scratch_shapes=[pltpu.VMEM((n_tiles, rows, VOCAB_BLOCK), jnp.float32)]
                       + [pltpu.VMEM((rows, LANES), jnp.float32)] * 4
                       + [pltpu.VMEM((8, width), jnp.float32), pltpu.VMEM((RING, 8, rows), jnp.float32)]
                       + [dma((len(PIECES), 4)), dma((4,)), dma((4,))] + [dma] * 7,
        compiler_params=pltpu.CompilerParams(
            vmem_limit_bytes=VMEM_LIMIT, collective_id=0, has_side_effects=True),
        cost_estimate=pl.CostEstimate(
            flops=60 * rows * vocab * width, bytes_accessed=vocab * 4 * width, transcendentals=2 * rows * vocab),
        name="exchange_tokens",
    )(h_act, h_wide, emb, local_ids, tgt_row)


def own_rows_kernel(inv_n, emb_ref, rid_ref, all_ref, h_ref, stats_ref, acc_ref):
    @pl.when(pl.program_id(0) == 0)
    def _():
        acc_ref[...] = jnp.zeros_like(acc_ref)

    blocks, rows = all_ref.shape[1], all_ref.shape[2] - 8
    h_blk = all_ref[0, :, :rows, :].reshape(blocks * rows, all_ref.shape[3]).astype(jnp.bfloat16)
    h_ref[...] = h_blk
    stats = jnp.concatenate([all_ref[0, i, rows:, :rows] for i in range(blocks)], axis=1)
    stats_ref[...] = stats
    logits = lax.dot_general(emb_ref[...], h_blk, NT, preferred_element_type=jnp.float32)
    prob = jnp.exp(logits - stats[0:1]) * stats[1:2]
    grad = prob - jnp.where(rid_ref[...] == stats[2:3], inv_n, 0.0)
    acc_ref[...] += jnp.dot(grad.astype(jnp.bfloat16), h_blk, preferred_element_type=jnp.float32)


def own_rows(emb, rid, gathered, inv_n):
    n_core, n_pos, n_in, width = gathered.shape
    n_own, n_tok = emb.shape[0], n_in - 8
    total = n_core * n_pos * n_tok
    per_core = n_pos // OWN_BLOCKS
    return pl.pallas_call(
        functools.partial(own_rows_kernel, inv_n),
        out_shape=(jax.ShapeDtypeStruct((total, width), jnp.bfloat16),
                   jax.ShapeDtypeStruct((8, total), jnp.float32),
                   jax.ShapeDtypeStruct((n_own, width), jnp.float32)),
        grid=(n_core * per_core,),
        in_specs=[pl.BlockSpec(memory_space=pltpu.VMEM), pl.BlockSpec(memory_space=pltpu.VMEM),
                  pl.BlockSpec((1, OWN_BLOCKS, n_in, width), lambda i: (i // per_core, lax.rem(i, per_core), 0, 0))],
        out_specs=(pl.BlockSpec((OWN_BLOCKS * n_tok, width), lambda i: (i, 0)),
                   pl.BlockSpec((8, OWN_BLOCKS * n_tok), lambda i: (0, i)),
                   pl.BlockSpec((n_own, width), lambda i: (0, 0))),
        compiler_params=pltpu.CompilerParams(vmem_limit_bytes=VMEM_LIMIT),
        cost_estimate=pl.CostEstimate(
            flops=4 * n_own * total * width, bytes_accessed=total * width * 6, transcendentals=n_own * total),
        name="own_rows",
    )(emb, rid, gathered)


def grad_rows_kernel(inv_n, emb_ref, rid_ref, h_ref, stats_ref, *refs):
    acc_ref = refs[-1]

    @pl.when(pl.program_id(1) == 0)
    def _():
        acc_ref[...] = jnp.zeros_like(acc_ref)

    h_blk = h_ref[...]
    logits = lax.dot_general(emb_ref[...], h_blk, NT, preferred_element_type=jnp.float32)
    prob = jnp.exp(logits - stats_ref[0:1, :]) * stats_ref[1:2, :]
    grad = prob - jnp.where(rid_ref[...] == stats_ref[2:3, :], inv_n, 0.0)
    acc_ref[...] += jnp.dot(grad.astype(jnp.bfloat16), h_blk, preferred_element_type=jnp.float32)


def grad_rows(emb, rid, h_all, stats, out, inv_n, n_out, first_block, n_blocks, row_block):
    width = emb.shape[1]
    n_tok = h_all.shape[0]
    tok_block = min(TOKEN_BLOCK, n_tok)
    in_specs = [
        pl.BlockSpec((row_block, width), lambda i, t: (i + first_block, 0)),
        pl.BlockSpec((row_block, 1), lambda i, t: (i + first_block, 0)),
        pl.BlockSpec((tok_block, width), lambda i, t: (t, 0)),
        pl.BlockSpec((8, tok_block), lambda i, t: (0, t)),
    ]
    args = [emb, rid, h_all, stats]
    if out is not None:
        in_specs.append(pl.BlockSpec(memory_space=pl.ANY))
        args.append(out)
    rows = n_blocks * row_block
    return pl.pallas_call(
        functools.partial(grad_rows_kernel, inv_n),
        out_shape=jax.ShapeDtypeStruct((n_out, width), jnp.float32),
        grid=(n_blocks, n_tok // tok_block),
        in_specs=in_specs,
        out_specs=pl.BlockSpec((row_block, width), lambda i, t: (i + first_block, 0)),
        input_output_aliases={4: 0} if out is not None else {},
        compiler_params=pltpu.CompilerParams(vmem_limit_bytes=VMEM_LIMIT),
        cost_estimate=pl.CostEstimate(
            flops=4 * rows * n_tok * width,
            bytes_accessed=rows * width * 6 + n_blocks * n_tok * width * 2,
            transcendentals=rows * n_tok),
        name="grad_rows",
    )(*args)


def place_kernel(src_ref, prev_ref, dst_ref):
    del prev_ref
    dst_ref[...] = src_ref[0, : dst_ref.shape[0], :]


def place_rows(gathered, n_rows, out, first_row):
    n_dev, n_in, width = gathered.shape
    first_block = first_row // n_rows
    return pl.pallas_call(
        place_kernel,
        out_shape=jax.ShapeDtypeStruct(out.shape, out.dtype),
        grid=(n_dev,),
        in_specs=[pl.BlockSpec((1, n_in, width), lambda i: (i, 0, 0)),
                  pl.BlockSpec(memory_space=pl.ANY)],
        out_specs=pl.BlockSpec((n_rows, width), lambda i: (i + first_block, 0)),
        input_output_aliases={1: 0},
        cost_estimate=pl.CostEstimate(
            flops=gathered.size * 80, bytes_accessed=gathered.size * 8, transcendentals=0),
        name="place_rows",
    )(gathered, out)


def shifts(n_tp):
    return [[(i, (i + shift) % n_tp) for i in range(n_tp)] for shift in range(1, n_tp)]


def send_blocks(part, n_tp, tp_idx):
    blocks = part.reshape(n_tp, part.shape[0] // n_tp, part.shape[1])
    pick = lambda i: lax.dynamic_index_in_dim(blocks, i % n_tp, 0, keepdims=False)
    return [pick(tp_idx)] + [lax.ppermute(pick(tp_idx + 1 + d), 'tp', perm) for d, perm in enumerate(shifts(n_tp))]


def send_total(blocks, n_tp):
    total = functools.reduce(jnp.add, blocks)
    return [total] + [lax.ppermute(total, 'tp', perm) for perm in shifts(n_tp)]


def join_totals(totals, n_tp, tp_idx):
    whole = jnp.zeros((n_tp,) + totals[0].shape, totals[0].dtype)
    for shift, total in enumerate(totals):
        whole = lax.dynamic_update_index_in_dim(whole, total, (tp_idx + n_tp - shift) % n_tp, 0)
    return whole.reshape(-1, totals[0].shape[1])


def solution(mesh):
    n_tp, n_dp = mesh.shape['tp'], mesh.shape['dp']

    def program(hidden, residual, targets, embedding, norm_w):
        inv_n = 1.0 / (hidden.shape[0] * hidden.shape[1])

        def local_part(hid_loc, res_loc, tgt_loc, emb_loc, norm_vec):
            n_batch, n_seq, d_model = hid_loc.shape
            n_rows = n_batch * n_seq
            vocab_loc = emb_loc.shape[0]
            tp_idx, dp_idx = lax.axis_index('tp'), lax.axis_index('dp')
            resid = (res_loc + hid_loc.astype(jnp.float32)).reshape(n_rows, d_model)
            tgt_rows = tgt_loc.reshape(n_rows)
            inv_rms = lax.rsqrt(jnp.mean(resid * resid, axis=-1, keepdims=True) + NORM_EPS)
            scaled_r = resid * inv_rms
            h_wide = lax.reduce_precision(scaled_r * norm_vec, exponent_bits=8, mantissa_bits=7)
            h_act = h_wide.astype(jnp.bfloat16)
            local_ids = (tgt_rows - tp_idx * vocab_loc)[:, None]
            local_ids = jnp.where(local_ids < vocab_loc, local_ids, -1)
            tgt_row = tgt_rows.astype(jnp.float32)[None]
            gathered, grad_h, stats = exchange_tokens(h_act, h_wide, emb_loc, local_ids, tgt_row, inv_n, n_dp)
            loss_part = jnp.sum(stats[0] + jnp.log(stats[3]) - stats[4]) * inv_n

            own_total = sum(GRAD_CHUNKS)
            split_rows = n_dp * own_total
            row_ids = (tp_idx * vocab_loc + jnp.arange(vocab_loc)).astype(jnp.float32)[:, None]
            own_emb, own_ids, base = [], [], 0
            for n_own in GRAD_CHUNKS:
                start = base + dp_idx * n_own
                own_emb.append(lax.dynamic_slice_in_dim(emb_loc, start, n_own))
                own_ids.append(lax.dynamic_slice_in_dim(row_ids, start, n_own))
                base += n_dp * n_own
            h_all, all_stats, own = own_rows(jnp.concatenate(own_emb), jnp.concatenate(own_ids), gathered, inv_n)
            grad_h, own = lax.optimization_barrier((grad_h, own))
            grad_h = send_blocks(grad_h, n_tp, tp_idx)

            first_block = split_rows // ROW_BLOCK
            n_blocks = -(-vocab_loc // ROW_BLOCK) - first_block
            out = None
            for c, n_part in enumerate((1, 1, n_blocks - 2)):
                out = grad_rows(emb_loc, row_ids, h_all, all_stats, out, inv_n, vocab_loc, first_block, n_part, ROW_BLOCK)
                first_block += n_part
                if c < 2:
                    grad_h, out = lax.optimization_barrier((grad_h, out))
                    grad_h = join_totals(grad_h, n_tp, tp_idx) if c else send_total(grad_h, n_tp)
            grad_scaled = grad_h * norm_vec
            grad_r = inv_rms * (grad_scaled - scaled_r * jnp.mean(grad_scaled * scaled_r, axis=-1, keepdims=True))
            grad_w = jnp.sum(grad_h * scaled_r, axis=0)

            first, base = 0, 0
            for c, n_own in enumerate(GRAD_CHUNKS):
                part = own[first:first + n_own]
                first += n_own
                if c == len(GRAD_CHUNKS) - 1:
                    sums = jnp.zeros((8, d_model), jnp.float32).at[0].set(grad_w).at[1, 0].set(loss_part)
                    part = jnp.concatenate([part, sums])
                got = lax.all_gather(part, 'dp')
                out = place_rows(got, n_own, out, base)
                base += n_dp * n_own
            sums = jnp.sum(got[:, n_own:n_own + 2], axis=0)
            return sums[1, 0], grad_r.reshape(n_batch, n_seq, d_model), out, sums[0]

        sharded = jax.shard_map(
            local_part, mesh=mesh,
            in_specs=(P('dp', None, None), P('dp', None, None), P('dp', None), P('tp', None), P(None)),
            out_specs=(P(), P('dp', None, None), P('tp', None), P(None)),
            check_vma=False)
        return sharded(hidden, residual, targets, embedding, norm_w)

    return program
```

profile of v0, /device:TPU:0, one launch (start us, length us, event | category | flops | bytes accessed | tf_op | source)
XLA Modules:
  0.0 801.9 jit_solution(196806807999682722)
XLA Ops:
  7.4 1.8 constant_dynamic-slice_fusion.1
  9.2 1.1 constant_dynamic-slice_fusion
  10.3 0.8 copy.20.rid_ref
  12.5 2.2 fusion.2
  14.7 1.4 pad_maximum_fusion.emb_ref
  16.2 2.4 fusion.5
  18.5 175.9 %exchange_tokens.1 = (f32[2,16,264,2560]{3,2,1,0:T(8,128)}, f32[256,2560]{1,0:T(8,128)}, f32[8,256]{1,0:T(8,128)}) custom-call(bf16[256,2560]{1,0:T(8,128)(2,1)} %get-tuple-element.66.h_ref, f32[256,2560]{1,0:T(8,128)} %get-tuple-element.67.own_ref, bf16[12572,2560]{1,0:T(8,128)(2,1)} %emb_ref.7, s32[256,1]{1,0:T(8,128)} %compare_select_fusion.ids_ref, ...), custom_call_target="tpu_custom_call" | custom-call | flops 494351155200 | bytes 128737280 | tf_op jit(solution)/shard_map/exchange_tokens/pallas_call | solution.py:293
  194.5 48.0 %own_rows.1 = (bf16[8192,2560]{1,0:T(8,128)(2,1)}, f32[8,8192]{1,0:T(8,128)}, f32[320,2560]{1,0:T(8,128)}) custom-call(bf16[320,2560]{1,0:T(8,128)(2,1)} %pad_maximum_fusion.emb_ref, f32[320,1]{1,0:T(8,128)} %copy.20.rid_ref, f32[2,16,264,2560]{3,2,1,0:T(8,128)} %get-tuple-element.47.all_ref), custom_call_target="tpu_custom_call" | custom-call | flops 26843545600 | bytes 125829120 | tf_op jit(solution)/shard_map/own_rows/pallas_call | solution.py:334
  242.5 1.5 dynamic-slice_bitcast_fusion
  244.5 2.1 collective-permute-start.1
  246.6 1.2 collective-permute-start.2
  247.8 3.0 add_convert_fusion.rid_ref
  250.8 51.8 %grad_rows.3.refs_0_ = f32[12572,2560]{1,0:T(8,128)} custom-call(bf16[12572,2560]{1,0:T(8,128)(2,1)} %emb_ref.7, f32[12572,1]{1,0:T(8,128)} %add_convert_fusion.rid_ref, bf16[8192,2560]{1,0:T(8,128)(2,1)} %get-tuple-element.51.h_ref, f32[8,8192]{1,0:T(8,128)} %get-tuple-element.52.stats_ref), custom_call_target="tpu_custom_call" | custom-call | flops 42949672960 | bytes 49807360 | tf_op jit(solution)/shard_map/grad_rows/pallas_call | solution.py:381
  302.6 1.1 slice.57
  303.7 1.4 subtract_reduce_fusion
  305.9 0.8 copy-done.12
  306.7 1.2 add_add_fusion
  307.9 1.0 collective-permute-start.3
  308.9 1.7 collective-permute-start.4
  310.5 2.5 collective-permute-start.5
  313.1 51.7 %grad_rows.4.refs_0_ = f32[12572,2560]{1,0:T(8,128)} custom-call(bf16[12572,2560]{1,0:T(8,128)(2,1)} %emb_ref.7, f32[12572,1]{1,0:T(8,128)} %add_convert_fusion.rid_ref, bf16[8192,2560]{1,0:T(8,128)(2,1)} %get-tuple-element.51.h_ref, f32[8,8192]{1,0:T(8,128)} %get-tuple-element.52.stats_ref, ...), custom_call_target="tpu_custom_call", output_to_operand_aliasing={{}: (4, {})} | custom-call | flops 42949672960 | bytes 49807360 | tf_op jit(solution)/shard_map/grad_rows/pallas_call | solution.py:381
  365.9 0.8 copy-done.10
  367.1 1.3 bitcast_dynamic-update-slice_fusion.2
  368.4 1.1 bitcast_dynamic-update-slice_fusion.1
  371.2 0.9 pad_maximum_fusion.1
  372.4 3.4 slice.63
  376.0 3.8 fusion.1
  379.8 143.8 %grad_rows.5.prev_ref = f32[12572,2560]{1,0:T(8,128)} custom-call(bf16[12572,2560]{1,0:T(8,128)(2,1)} %emb_ref.7, f32[12572,1]{1,0:T(8,128)} %add_convert_fusion.rid_ref, bf16[8192,2560]{1,0:T(8,128)(2,1)} %get-tuple-element.51.h_ref, f32[8,8192]{1,0:T(8,128)} %get-tuple-element.52.stats_ref, ...), custom_call_target="tpu_custom_call", output_to_operand_aliasing={{}: (4, {})} | custom-call | flops 128849018880 | bytes 149422080 | tf_op jit(solution)/shard_map/grad_rows/pallas_call | solution.py:381
  523.6 1.9 slice_reduce_fusion
  526.7 177.2 %all-gather.7.cloned.1.call-done = f32[8192,2560]{1,0:T(8,128)} async-done(((f32[256,2560]{1,0:T(8,128)}), f32[8192,2560]{1,0:T(8,128)}) %all-gather.7.cloned.1.call-update) | async-done | bytes 83886096 | tf_op jit(solution)/shard_map/all_gather | solution.py:497
  703.9 63.3 %place_rows.2.prev_ref = f32[12572,2560]{1,0:T(8,128)} custom-call(f32[32,256,2560]{2,1,0:T(8,128)} %bitcast.18.src_ref, f32[12572,2560]{1,0:T(8,128)} %grad_rows.5.prev_ref), custom_call_target="tpu_custom_call", output_to_operand_aliasing={{}: (1, {})} | custom-call | flops 1677721600 | bytes 167772160 | tf_op jit(solution)/shard_map/place_rows/pallas_call | solution.py:405
  767.2 27.9 %place_rows.3 = f32[12572,2560]{1,0:T(8,128)} custom-call(f32[32,72,2560]{2,1,0:T(8,128)} %bitcast.46, f32[12572,2560]{1,0:T(8,128)} %place_rows.2.prev_ref), custom_call_target="tpu_custom_call", output_to_operand_aliasing={{}: (1, {})} | custom-call | flops 471859200 | bytes 47185920 | tf_op jit(solution)/shard_map/place_rows/pallas_call | solution.py:405
  (66 shorter events, 6.7 us)
Async XLA Ops:
  7.2 4.0 copy-start.17
  7.2 5.3 copy-start.7
  7.2 516.4 %all-gather.5.cloned.1.call-start = ((), (), s32[]{:S(2)}) async-start(), calls=%async_computation | async-start | bytes 24330240 | tf_op jit(solution)/shard_map/all_gather | solution.py:497
  14.7 3.8 copy-start
  14.7 1.5 copy-start.13
  14.7 3.8 copy-start.15
  194.5 48.0 %copy-start.3 = (f32[256,2560]{1,0:T(8,128)S(1)}, f32[256,2560]{1,0:T(8,128)}, u32[]{:S(2)}) copy-start(f32[256,2560]{1,0:T(8,128)} %get-tuple-element.50) | copy-start | bytes 7864324
  244.0 61.8 %collective-permute-start = (f32[64,2560]{1,0:T(8,128)}, f32[64,2560]{1,0:T(8,128)S(1)}, u32[]{:S(2)}, u32[]{:S(2)}) collective-permute-start(f32[64,2560]{1,0:T(8,128)} %get-tuple-element.72), channel_id=1, source_target_pairs={{0,32},{32,64},{64,96},{96,0},{1,33},{33,65},{65,97},{97,1},{2,34}... | collective-permute-start | bytes 1966088 | tf_op jit(solution)/shard_map/ppermute | solution.py:426
  244.5 61.3 %collective-permute-start.1 = (f32[64,2560]{1,0:T(8,128)}, f32[64,2560]{1,0:T(8,128)S(1)}, u32[]{:S(2)}, u32[]{:S(2)}) collective-permute-start(f32[64,2560]{1,0:T(8,128)} %get-tuple-element.71), channel_id=1, source_target_pairs={{0,64},{32,96},{64,0},{96,32},{1,65},{33,97},{65,1},{97,33},{2,66}... | collective-permute-start | bytes 1966088 | tf_op jit(solution)/shard_map/ppermute | solution.py:426
  246.6 59.2 %collective-permute-start.2 = (f32[64,2560]{1,0:T(8,128)}, f32[64,2560]{1,0:T(8,128)S(1)}, u32[]{:S(2)}, u32[]{:S(2)}) collective-permute-start(f32[64,2560]{1,0:T(8,128)} %get-tuple-element.70), channel_id=1, source_target_pairs={{0,96},{32,0},{64,32},{96,64},{1,97},{33,1},{65,33},{97,65},{2,98}... | collective-permute-start | bytes 1966088 | tf_op jit(solution)/shard_map/ppermute | solution.py:426
  250.8 51.8 %copy-start.16 = (f32[256]{0:T(256)S(1)}, f32[256]{0:T(256)}, u32[]{:S(2)}) copy-start(f32[256]{0:T(256)} %copy-done.15) | copy-start | bytes 3076
  250.8 55.9 %copy-start.4 = (f32[64,2560]{1,0:T(8,128)S(1)}, f32[64,2560]{1,0:T(8,128)}, u32[]{:S(2)}) copy-start(f32[64,2560]{1,0:T(8,128)} %get-tuple-element.53) | copy-start | bytes 1966084
  305.9 0.8 copy-start.12
  307.9 56.9 %copy-start.5 = (f32[64,2560]{1,0:T(8,128)}, f32[64,2560]{1,0:T(8,128)S(1)}, u32[]{:S(2)}) copy-start(f32[64,2560]{1,0:T(8,128)S(1)} %add_add_fusion) | copy-start | bytes 1966084
  307.9 56.9 %collective-permute-start.3 = (f32[64,2560]{1,0:T(8,128)S(1)}, f32[64,2560]{1,0:T(8,128)S(1)}, u32[]{:S(2)}, u32[]{:S(2)}) collective-permute-start(f32[64,2560]{1,0:T(8,128)S(1)} %add_add_fusion), channel_id=1, source_target_pairs={{0,32},{32,64},{64,96},{96,0},{1,33},{33,65},{65,97},{97,1},{2,34}... | collective-permute-start | bytes 1966088 | tf_op jit(solution)/shard_map/ppermute | solution.py:431
  308.9 56.0 %collective-permute-start.4 = (f32[64,2560]{1,0:T(8,128)S(1)}, f32[64,2560]{1,0:T(8,128)S(1)}, u32[]{:S(2)}, u32[]{:S(2)}) collective-permute-start(f32[64,2560]{1,0:T(8,128)S(1)} %add_add_fusion), channel_id=1, source_target_pairs={{0,64},{32,96},{64,0},{96,32},{1,65},{33,97},{65,1},{97,33},{2,66}... | collective-permute-start | bytes 1966088 | tf_op jit(solution)/shard_map/ppermute | solution.py:431
  310.5 54.3 %collective-permute-start.5 = (f32[64,2560]{1,0:T(8,128)S(1)}, f32[64,2560]{1,0:T(8,128)S(1)}, u32[]{:S(2)}, u32[]{:S(2)}) collective-permute-start(f32[64,2560]{1,0:T(8,128)S(1)} %add_add_fusion), channel_id=1, source_target_pairs={{0,96},{32,0},{64,32},{96,64},{1,97},{33,1},{65,33},{97,65},{2,98}... | collective-permute-start | bytes 1966088 | tf_op jit(solution)/shard_map/ppermute | solution.py:431
  364.8 0.9 copy-start.8
  364.8 2.2 copy-start.6
  364.8 1.1 copy-start.9
  365.9 0.8 copy-start.10
  367.0 2.5 copy-start.11
  367.0 2.6 copy-start.1
  367.0 2.6 copy-start.14
  369.6 1.5 copy-start.2
  372.2 331.7 %all-gather.7.cloned.1.call-start = ((), (), s32[]{:S(2)}) async-start(), calls=%async_computation.1 | async-start | bytes 86507520 | tf_op jit(solution)/shard_map/all_gather | solution.py:497
Sparse Core Ops, SparseCore 0:
  372.3 85.1 all-gather.4
  459.8 244.0 all-gather.6
where the time goes:
time: 805 us; the launch traced here: 802 us
  Pallas kernels  562 us (70%)
  waiting for transfers between devices  177 us (22%)
  other arithmetic  20.1 us (2%)
  local copies, waits for them, and re-layouts  17.8 us (2%)
  between operations  15.1 us (2%)
  starting transfers between devices  9.19 us (1%)
    pallas_call x3, Pallas kernels, grad_rows(): pl.pallas_call(functools.partial(grad_rows_kernel, inv_n), out_shape=jax....  247 us
    all_gather x2, waiting for transfers between devices, local_part(): got = lax.all_gather(part, 'dp')  177 us
    pallas_call x1, Pallas kernels, exchange_tokens(): pl.pallas_call(functools.partial(exchange_kernel, plan, PIECES, SHARE_ROW...  176 us
    pallas_call x2, Pallas kernels, place_rows(): pl.pallas_call(place_kernel, out_shape=jax.ShapeDtypeStruct(out.shape, ou...  91.2 us
    pallas_call x1, Pallas kernels, own_rows(): pl.pallas_call(functools.partial(own_rows_kernel, inv_n), out_shape=(jax....  48 us
  transfers between devices with their start and end apart: 8, of which 1 were waited for; matrix products, arithmetic and copies ran while one was open for 2% of the time, Pallas kernels for 31%

commit v1 on v0

--- a/solution.py
+++ b/solution.py
@@ -14,16 +14,36 @@
 NT = (((1,), (1,)), ((), ()))
 SHARE_ROWS = 24
 PIECES = (('share', 0, 24), ('direct', 96, 40), ('direct', 136, 40), ('direct', 176, 40), ('direct', 216, 40), ('stats', 256, 8))
-PLAN = ((('start', 0), ('start', 1)), (), (), (('start', 2), ('r', 0, 1)), (), (), (('r', 1, 1),), (), (), (), (('r', 2, 1),),
- (('start', 5),), (('x', 1), ('r', 0, 2)), (), (), (), (), (('r', 1, 2), ('f', 1)), (), (),
- (('r', 2, 2), ('r', 5, 1), ('r', 0, 3), ('r', 1, 3), ('x', 2), ('start', 3), ('r', 2, 3), ('r', 5, 2), ('r', 0, 4),
-  ('r', 1, 4), ('start', 4), ('r', 3, 1), ('x', 3), ('r', 2, 4), ('r', 5, 3), ('r', 4, 1), ('f', 2), ('x', 4),
-  ('r', 3, 2), ('r', 5, 4), ('f', 3), ('f', 4), ('r', 4, 2), ('r', 3, 3), ('r', 4, 3), ('r', 3, 4), ('r', 4, 4)))
+PLAN = (
+    ('s0,s1',),
+    (),
+    (),
+    ('s2,r01',),
+    (),
+    (),
+    ('r11',),
+    (),
+    (),
+    (),
+    ('r21',),
+    ('s5',),
+    ('x1,r02',),
+    (),
+    (),
+    (),
+    (),
+    ('r12,f1',),
+    (),
+    (),
+    ('r22,r51,r03,r13,x2,s3,r23,r52,r04,r14,s4,r31,x3,r24', 'r53,r41,f2,x4,r32,r54,f3,f4,r42,r33,r43,r34,r44'),
+)
 VOCAB_BLOCK = 1280
-GRAD_CHUNKS = (256, 64)
+GRAD_CHUNKS = (144, 96)
 ROW_BLOCK = 512
+BLOCK_CALLS = (1, 1, 1, 2)
 TOKEN_BLOCK = 1024
-OWN_BLOCKS = 2
+POS_BLOCK = 2
+PLACE_BLOCK = 4
 
 
 RING = 4
@@ -183,19 +203,22 @@
     ex = Exchange(own_ref, stats_ref, all_ref, sems, share_rows)
 
     def run(event):
-        if event[0] == 'start':
-            ex.round(event[1], pieces[event[1]], 1)
-        elif event[0] == 'r':
-            _, p, k = event
+        kind, *nums = event
+        nums = [int(v) for v in nums]
+        if kind == 's':
+            ex.round(nums[0], pieces[nums[0]], 1)
+        elif kind == 'r':
+            p, k = nums
             ex.finish_round(p, pieces[p], k)
             if k < 4:
                 ex.round(p, pieces[p], k + 1)
-        elif event[0] == 'x':
-            ex.along_x(event[1])
+        elif kind == 'x':
+            ex.along_x(nums[0])
         else:
-            ex.finish_x(event[1])
-
-    for i, events in enumerate(plan):
+            ex.finish_x(nums[0])
+
+    for i, groups in enumerate(plan):
+        events = [event for group in groups for event in group.split(',')]
         if events:
             @pl.when(step == i)
             def _(i=i, events=events):
@@ -310,110 +333,262 @@
     )(h_act, h_wide, emb, local_ids, tgt_row)
 
 
-def own_rows_kernel(inv_n, emb_ref, rid_ref, all_ref, h_ref, stats_ref, acc_ref):
-    @pl.when(pl.program_id(0) == 0)
-    def _():
-        acc_ref[...] = jnp.zeros_like(acc_ref)
-
+def row_grads(inv_n, emb, row_ids, h_blk, stats):
+    logits = lax.dot_general(emb, h_blk, NT, preferred_element_type=jnp.float32)
+    prob = jnp.exp(logits - stats[0:1]) * stats[1:2]
+    grad = prob - jnp.where(row_ids == stats[2:3], inv_n, 0.0)
+    return jnp.dot(grad.astype(jnp.bfloat16), h_blk, preferred_element_type=jnp.float32)
+
+
+def id_column(n_rows, first):
+    return (lax.broadcasted_iota(jnp.int32, (n_rows, 1), 0) + first).astype(jnp.float32)
+
+
+def load_tokens(all_ref):
     blocks, rows = all_ref.shape[1], all_ref.shape[2] - 8
     h_blk = all_ref[0, :, :rows, :].reshape(blocks * rows, all_ref.shape[3]).astype(jnp.bfloat16)
-    h_ref[...] = h_blk
-    stats = jnp.concatenate([all_ref[0, i, rows:, :rows] for i in range(blocks)], axis=1)
-    stats_ref[...] = stats
-    logits = lax.dot_general(emb_ref[...], h_blk, NT, preferred_element_type=jnp.float32)
-    prob = jnp.exp(logits - stats[0:1]) * stats[1:2]
-    grad = prob - jnp.where(rid_ref[...] == stats[2:3], inv_n, 0.0)
-    acc_ref[...] += jnp.dot(grad.astype(jnp.bfloat16), h_blk, preferred_element_type=jnp.float32)
-
-
-def own_rows(emb, rid, gathered, inv_n):
-    n_core, n_pos, n_in, width = gathered.shape
-    n_own, n_tok = emb.shape[0], n_in - 8
-    total = n_core * n_pos * n_tok
-    per_core = n_pos // OWN_BLOCKS
+    return h_blk, jnp.concatenate([all_ref[0, i, rows:, :rows] for i in range(blocks)], axis=1)
+
+
+def token_spec(gathered):
+    _, n_pos, n_in, width = gathered.shape
+    per_core = n_pos // POS_BLOCK
+    return pl.BlockSpec((1, POS_BLOCK, n_in, width), lambda i, where: (i // per_core, lax.rem(i, per_core), 0, 0))
+
+
+def own_rows_kernel(inv_n, bases, where, emb0_ref, emb1_ref, all_ref, own0_ref, own1_ref, emb_ref, acc_ref):
+    n0, n1 = emb0_ref.shape[0], emb1_ref.shape[0]
+
+    @pl.when(pl.program_id(0) == 0)
+    def _():
+        emb_ref[:n0] = emb0_ref[...]
+        emb_ref[n0:] = emb1_ref[...]
+        acc_ref[...] = jnp.zeros_like(acc_ref)
+
+    first0, first1 = [where[1] + base + where[0] * n for base, n in zip(bases, (n0, n1))]
+    row = lax.broadcasted_iota(jnp.int32, (n0 + n1, 1), 0)
+    row_ids = (row + jnp.where(row < n0, first0, first1 - n0)).astype(jnp.float32)
+    h_blk, stats = load_tokens(all_ref)
+    acc_ref[...] += row_grads(inv_n, emb_ref[...], row_ids, h_blk, stats)
+
+    @pl.when(pl.program_id(0) == pl.num_programs(0) - 1)
+    def _():
+        own0_ref[...] = acc_ref[:n0]
+        own1_ref[:n1] = acc_ref[n0:]
+        own1_ref[n1:] = jnp.zeros_like(own1_ref[n1:])
+
+
+def own_rows(emb, gathered, where, inv_n, n_dp):
+    width = emb.shape[1]
+    n_tok = gathered.shape[0] * gathered.shape[1] * (gathered.shape[2] - 8)
+    n0, n1 = GRAD_CHUNKS
+    bases = (0, n_dp * n0)
+    emb_spec = lambda base, n: pl.BlockSpec((n, width), lambda i, where: (base // n + where[0], 0))
+    whole = lambda n: pl.BlockSpec((n, width), lambda i, where: (0, 0))
     return pl.pallas_call(
-        functools.partial(own_rows_kernel, inv_n),
-        out_shape=(jax.ShapeDtypeStruct((total, width), jnp.bfloat16),
-                   jax.ShapeDtypeStruct((8, total), jnp.float32),
-                   jax.ShapeDtypeStruct((n_own, width), jnp.float32)),
-        grid=(n_core * per_core,),
-        in_specs=[pl.BlockSpec(memory_space=pltpu.VMEM), pl.BlockSpec(memory_space=pltpu.VMEM),
-                  pl.BlockSpec((1, OWN_BLOCKS, n_in, width), lambda i: (i // per_core, lax.rem(i, per_core), 0, 0))],
-        out_specs=(pl.BlockSpec((OWN_BLOCKS * n_tok, width), lambda i: (i, 0)),
-                   pl.BlockSpec((8, OWN_BLOCKS * n_tok), lambda i: (0, i)),
-                   pl.BlockSpec((n_own, width), lambda i: (0, 0))),
+        functools.partial(own_rows_kernel, inv_n, bases),
+        out_shape=(jax.ShapeDtypeStruct((n0, width), jnp.float32), jax.ShapeDtypeStruct((n1 + 8, width), jnp.float32)),
+        grid_spec=pltpu.PrefetchScalarGridSpec(
+            num_scalar_prefetch=1,
+            grid=(gathered.shape[0] * gathered.shape[1] // POS_BLOCK,),
+            in_specs=[emb_spec(bases[0], n0), emb_spec(bases[1], n1), token_spec(gathered)],
+            out_specs=(whole(n0), whole(n1 + 8)),
+            scratch_shapes=[pltpu.VMEM((n0 + n1, width), jnp.bfloat16), pltpu.VMEM((n0 + n1, width), jnp.float32)]),
         compiler_params=pltpu.CompilerParams(vmem_limit_bytes=VMEM_LIMIT),
         cost_estimate=pl.CostEstimate(
-            flops=4 * n_own * total * width, bytes_accessed=total * width * 6, transcendentals=n_own * total),
+            flops=4 * (n0 + n1) * n_tok * width, bytes_accessed=n_tok * width * 4, transcendentals=(n0 + n1) * n_tok),
         name="own_rows",
-    )(emb, rid, gathered)
-
-
-def grad_rows_kernel(inv_n, emb_ref, rid_ref, h_ref, stats_ref, *refs):
-    acc_ref = refs[-1]
-
-    @pl.when(pl.program_id(1) == 0)
+    )(where, emb, emb, gathered)
+
+
+def first_block_kernel(inv_n, first, where, emb_ref, all_ref, out_ref, copy_ref, h_ref, stats_ref):
+    step, last = pl.program_id(0), pl.num_programs(0) - 1
+
+    @pl.when(step == 0)
+    def _():
+        out_ref[...] = jnp.zeros_like(out_ref)
+
+    h_blk, stats = load_tokens(all_ref)
+    h_ref[...] = h_blk
+    stats_ref[...] = stats
+    n_rows = emb_ref.shape[0]
+    row_ids = id_column(n_rows, where[1] + (where[2] + first) * n_rows)
+    out_ref[...] += row_grads(inv_n, emb_ref[...], row_ids, h_blk, stats)
+
+    @pl.when(step == last)
+    def _():
+        copy_ref[...] = out_ref[...]
+
+
+def first_block(emb, gathered, where, inv_n, first):
+    vocab, width = emb.shape
+    n_tok = gathered.shape[0] * gathered.shape[1] * (gathered.shape[2] - 8)
+    per_step = POS_BLOCK * (gathered.shape[2] - 8)
+    row_spec = pl.BlockSpec((ROW_BLOCK, width), lambda i, where: (first + where[2], 0))
+    return pl.pallas_call(
+        functools.partial(first_block_kernel, inv_n, first),
+        out_shape=(jax.ShapeDtypeStruct((vocab, width), jnp.float32),
+                   jax.ShapeDtypeStruct((ROW_BLOCK, width), jnp.float32),
+                   jax.ShapeDtypeStruct((n_tok, width), jnp.bfloat16),
+                   jax.ShapeDtypeStruct((8, n_tok), jnp.float32)),
+        grid_spec=pltpu.PrefetchScalarGridSpec(
+            num_scalar_prefetch=1,
+            grid=(n_tok // per_step,),
+            in_specs=[row_spec, token_spec(gathered)],
+            out_specs=(row_spec, pl.BlockSpec((ROW_BLOCK, width), lambda i, where: (0, 0)),
+                       pl.BlockSpec((per_step, width), lambda i, where: (i, 0)),
+                       pl.BlockSpec((8, per_step), lambda i, where: (0, i)))),
+        compiler_params=pltpu.CompilerParams(vmem_limit_bytes=VMEM_LIMIT),
+        cost_estimate=pl.CostEstimate(
+            flops=4 * ROW_BLOCK * n_tok * width, bytes_accessed=n_tok * width * 6, transcendentals=ROW_BLOCK * n_tok),
+        name="first_block",
+    )(where, emb, gathered)
+
+
+class Placing:
+    def __init__(self, out_ref, got_ref, recv_refs, recv_rows, n_steps, stages, sems):
+        self.out_ref, self.got_ref, self.recv_refs, self.recv_rows = out_ref, got_ref, recv_refs, recv_rows
+        self.n_steps, self.stages, self.sems = n_steps, stages, sems
+        self.per_step = got_ref.shape[0] // n_steps
+        self.n_got = stages[0].shape[2]
+        self.n_recv = stages[1].shape[1]
+        self.parts = recv_refs[0].shape[0] // self.n_recv
+
+    def copies(self, step, slot, store):
+        sem = self.sems.at[1 if store else 0, slot]
+        for j in range(self.per_step):
+            i = step * self.per_step + j
+            stage = self.stages[0].at[slot, j]
+            if store:
+                yield pltpu.make_async_copy(stage, self.out_ref.at[pl.ds(pl.multiple_of(i * self.n_got, 8), self.n_got)], sem)
+            else:
+                yield pltpu.make_async_copy(self.got_ref.at[i, pl.ds(0, self.n_got)], stage, sem)
+
+    def recv_copy(self, step, slot, store, k):
+        sem = self.sems.at[3 if store else 2, slot]
+        part = (step - k * self.parts) * self.n_recv
+        stage = self.stages[1].at[slot]
+        if store:
+            row = pl.multiple_of(self.recv_rows[k] + part, 8)
+            return pltpu.make_async_copy(stage, self.out_ref.at[pl.ds(row, self.n_recv)], sem)
+        return pltpu.make_async_copy(self.recv_refs[k].at[pl.ds(pl.multiple_of(part, 8), self.n_recv)], stage, sem)
+
+    def each(self, step, store, act):
+        slot = lax.rem(step, 2)
+        for copy in self.copies(step, slot, store):
+            act(copy)
+        for k in range(len(self.recv_refs)):
+            @pl.when(jnp.logical_and(step >= k * self.parts, step < (k + 1) * self.parts))
+            def _(k=k):
+                act(self.recv_copy(step, slot, store, k))
+
+    def before(self, step):
+        @pl.when(step >= 1)
+        def _():
+            self.each(step - 1, False, lambda c: c.wait())
+            self.each(step - 1, True, lambda c: c.start())
+
+        @pl.when(step >= 2)
+        def _():
+            self.each(step - 2, True, lambda c: c.wait())
+
+        self.each(step, False, lambda c: c.start())
+
+    def after(self, step):
+        @pl.when(step == self.n_steps - 1)
+        def _():
+            self.each(step, False, lambda c: c.wait())
+            self.each(step, True, lambda c: c.start())
+            self.each(step - 1, True, lambda c: c.wait())
+            self.each(step, True, lambda c: c.wait())
+
+
+def grad_rows_kernel(inv_n, first, n_steps, recv_firsts, where, emb_ref, h_ref, stats_ref, *refs):
+    i, t = pl.program_id(0), pl.program_id(1)
+    n_ref = 2 + len(recv_firsts) if recv_firsts else 1
+    out_in_ref, acc_ref, copy_ref = refs[0], refs[n_ref], refs[n_ref + 1]
+    n_rows = emb_ref.shape[0]
+    placing = None
+    if recv_firsts:
+        rows = [(where[3] + block) * n_rows for block in recv_firsts]
+        placing = Placing(out_in_ref, refs[1], refs[2:n_ref], rows, n_steps, refs[n_ref + 2:n_ref + 4], refs[n_ref + 4])
+        placing.before(i * pl.num_programs(1) + t)
+
+    @pl.when(t == 0)
     def _():
         acc_ref[...] = jnp.zeros_like(acc_ref)
 
-    h_blk = h_ref[...]
-    logits = lax.dot_general(emb_ref[...], h_blk, NT, preferred_element_type=jnp.float32)
-    prob = jnp.exp(logits - stats_ref[0:1, :]) * stats_ref[1:2, :]
-    grad = prob - jnp.where(rid_ref[...] == stats_ref[2:3, :], inv_n, 0.0)
-    acc_ref[...] += jnp.dot(grad.astype(jnp.bfloat16), h_blk, preferred_element_type=jnp.float32)
-
-
-def grad_rows(emb, rid, h_all, stats, out, inv_n, n_out, first_block, n_blocks, row_block):
-    width = emb.shape[1]
+    row_ids = id_column(n_rows, where[1] + (where[2] + first + i) * n_rows)
+    acc_ref[...] += row_grads(inv_n, emb_ref[...], row_ids, h_ref[...], stats_ref[...])
+
+    @pl.when(t == pl.num_programs(1) - 1)
+    def _():
+        copy_ref[...] = acc_ref[...]
+
+    if placing:
+        placing.after(i * pl.num_programs(1) + t)
+
+
+def grad_rows(emb, h_all, stats, where, out, inv_n, first, n_blocks, got=None, n_got=0, recvs=(), recv_firsts=()):
+    vocab, width = emb.shape
     n_tok = h_all.shape[0]
     tok_block = min(TOKEN_BLOCK, n_tok)
-    in_specs = [
-        pl.BlockSpec((row_block, width), lambda i, t: (i + first_block, 0)),
-        pl.BlockSpec((row_block, 1), lambda i, t: (i + first_block, 0)),
-        pl.BlockSpec((tok_block, width), lambda i, t: (t, 0)),
-        pl.BlockSpec((8, tok_block), lambda i, t: (0, t)),
-    ]
-    args = [emb, rid, h_all, stats]
-    if out is not None:
-        in_specs.append(pl.BlockSpec(memory_space=pl.ANY))
-        args.append(out)
-    rows = n_blocks * row_block
+    n_steps = n_blocks * (n_tok // tok_block)
+    row_spec = pl.BlockSpec((ROW_BLOCK, width), lambda i, t, where: (i + first + where[2], 0))
+    anywhere = pl.BlockSpec(memory_space=pl.ANY)
+    in_specs = [row_spec, pl.BlockSpec((tok_block, width), lambda i, t, where: (t, 0)),
+                pl.BlockSpec((8, tok_block), lambda i, t, where: (0, t)), anywhere]
+    args, scratch = [emb, h_all, stats, out], []
+    if recvs:
+        args += [got, *recvs]
+        in_specs += [anywhere] * (1 + len(recvs))
+        part = ROW_BLOCK * len(recvs) // n_steps
+        part = next(n for n in range(max(part, 8), ROW_BLOCK + 1, 8) if ROW_BLOCK % n == 0 and n * n_steps >= ROW_BLOCK * len(recvs))
+        scratch = [pltpu.VMEM((2, got.shape[0] // n_steps, n_got, width), jnp.float32),
+                   pltpu.VMEM((2, part, width), jnp.float32), pltpu.SemaphoreType.DMA((4, 2))]
+    rows = n_blocks * ROW_BLOCK
     return pl.pallas_call(
-        functools.partial(grad_rows_kernel, inv_n),
-        out_shape=jax.ShapeDtypeStruct((n_out, width), jnp.float32),
-        grid=(n_blocks, n_tok // tok_block),
-        in_specs=in_specs,
-        out_specs=pl.BlockSpec((row_block, width), lambda i, t: (i + first_block, 0)),
-        input_output_aliases={4: 0} if out is not None else {},
+        functools.partial(grad_rows_kernel, inv_n, first, n_steps, tuple(recv_firsts)),
+        out_shape=(jax.ShapeDtypeStruct((vocab, width), jnp.float32), jax.ShapeDtypeStruct((rows, width), jnp.float32)),
+        grid_spec=pltpu.PrefetchScalarGridSpec(
+            num_scalar_prefetch=1,
+            grid=(n_blocks, n_tok // tok_block),
+            in_specs=in_specs,
+            out_specs=(row_spec, pl.BlockSpec((ROW_BLOCK, width), lambda i, t, where: (i, 0))),
+            scratch_shapes=scratch),
+        input_output_aliases={4: 0},
         compiler_params=pltpu.CompilerParams(vmem_limit_bytes=VMEM_LIMIT),
         cost_estimate=pl.CostEstimate(
             flops=4 * rows * n_tok * width,
             bytes_accessed=rows * width * 6 + n_blocks * n_tok * width * 2,
             transcendentals=rows * n_tok),
         name="grad_rows",
-    )(*args)
-
-
-def place_kernel(src_ref, prev_ref, dst_ref):
-    del prev_ref
-    dst_ref[...] = src_ref[0, : dst_ref.shape[0], :]
-
-
-def place_rows(gathered, n_rows, out, first_row):
-    n_dev, n_in, width = gathered.shape
-    first_block = first_row // n_rows
+    )(where, *args)
+
+
+def place_kernel(where, src_ref, prev_ref, dst_ref):
+    del where, prev_ref
+    n_dev, n_rows = src_ref.shape[0], dst_ref.shape[0] // src_ref.shape[0]
+    for i in range(n_dev):
+        dst_ref[i * n_rows:(i + 1) * n_rows] = src_ref[i, :n_rows]
+
+
+def place_rows(src, n_rows, out, where, first_block, per_block):
+    n_src, n_in, width = src.shape
     return pl.pallas_call(
         place_kernel,
         out_shape=jax.ShapeDtypeStruct(out.shape, out.dtype),
-        grid=(n_dev,),
-        in_specs=[pl.BlockSpec((1, n_in, width), lambda i: (i, 0, 0)),
-                  pl.BlockSpec(memory_space=pl.ANY)],
-        out_specs=pl.BlockSpec((n_rows, width), lambda i: (i + first_block, 0)),
-        input_output_aliases={1: 0},
-        cost_estimate=pl.CostEstimate(
-            flops=gathered.size * 80, bytes_accessed=gathered.size * 8, transcendentals=0),
+        grid_spec=pltpu.PrefetchScalarGridSpec(
+            num_scalar_prefetch=1,
+            grid=(n_src // per_block,),
+            in_specs=[pl.BlockSpec((per_block, n_in, width), lambda i, where: (i, 0, 0)),
+                      pl.BlockSpec(memory_space=pl.ANY)],
+            out_specs=pl.BlockSpec((per_block * n_rows, width), lambda i, where: (i + first_block + where[3], 0))),
+        input_output_aliases={2: 0},
+        compiler_params=pltpu.CompilerParams(vmem_limit_bytes=VMEM_LIMIT),
+        cost_estimate=pl.CostEstimate(flops=src.size * 80, bytes_accessed=src.size * 8, transcendentals=0),
         name="place_rows",
-    )(gathered, out)
+    )(where, src, out)
 
 
 def shifts(n_tp):
@@ -461,43 +636,47 @@
             gathered, grad_h, stats = exchange_tokens(h_act, h_wide, emb_loc, local_ids, tgt_row, inv_n, n_dp)
             loss_part = jnp.sum(stats[0] + jnp.log(stats[3]) - stats[4]) * inv_n
 
-            own_total = sum(GRAD_CHUNKS)
-            split_rows = n_dp * own_total
-            row_ids = (tp_idx * vocab_loc + jnp.arange(vocab_loc)).astype(jnp.float32)[:, None]
-            own_emb, own_ids, base = [], [], 0
-            for n_own in GRAD_CHUNKS:
-                start = base + dp_idx * n_own
-                own_emb.append(lax.dynamic_slice_in_dim(emb_loc, start, n_own))
-                own_ids.append(lax.dynamic_slice_in_dim(row_ids, start, n_own))
-                base += n_dp * n_own
-            h_all, all_stats, own = own_rows(jnp.concatenate(own_emb), jnp.concatenate(own_ids), gathered, inv_n)
-            grad_h, own = lax.optimization_barrier((grad_h, own))
+            per_core = sum(BLOCK_CALLS)
+            core = dp_idx % 2
+            where = jnp.stack([dp_idx, tp_idx * vocab_loc, core * per_core, (1 - core) * per_core]).astype(jnp.int32)
+            own0, own1 = own_rows(emb_loc, gathered, where, inv_n, n_dp)
+            got0 = lax.all_gather(own0, 'dp')
+            gathered, grad_h, own0 = lax.optimization_barrier((gathered, grad_h, own0))
             grad_h = send_blocks(grad_h, n_tp, tp_idx)
 
-            first_block = split_rows // ROW_BLOCK
-            n_blocks = -(-vocab_loc // ROW_BLOCK) - first_block
-            out = None
-            for c, n_part in enumerate((1, 1, n_blocks - 2)):
-                out = grad_rows(emb_loc, row_ids, h_all, all_stats, out, inv_n, vocab_loc, first_block, n_part, ROW_BLOCK)
-                first_block += n_part
+            first = n_dp * sum(GRAD_CHUNKS) // ROW_BLOCK
+            pair = [(i, i ^ 1) for i in range(n_dp)]
+            out, copied, h_all, all_stats = first_block(emb_loc, gathered, where, inv_n, first)
+            recvs, recv_firsts, late, block = [], [], [], first
+            for c, n_blocks in enumerate(BLOCK_CALLS):
+                final = c == len(BLOCK_CALLS) - 1
+                if c:
+                    extra = (got0, GRAD_CHUNKS[0], recvs, recv_firsts) if final else ()
+                    out, copied = grad_rows(emb_loc, h_all, all_stats, where, out, inv_n, block, n_blocks, *extra)
                 if c < 2:
                     grad_h, out = lax.optimization_barrier((grad_h, out))
                     grad_h = join_totals(grad_h, n_tp, tp_idx) if c else send_total(grad_h, n_tp)
-            grad_scaled = grad_h * norm_vec
-            grad_r = inv_rms * (grad_scaled - scaled_r * jnp.mean(grad_scaled * scaled_r, axis=-1, keepdims=True))
-            grad_w = jnp.sum(grad_h * scaled_r, axis=0)
-
-            first, base = 0, 0
-            for c, n_own in enumerate(GRAD_CHUNKS):
-                part = own[first:first + n_own]
-                first += n_own
-                if c == len(GRAD_CHUNKS) - 1:
-                    sums = jnp.zeros((8, d_model), jnp.float32).at[0].set(grad_w).at[1, 0].set(loss_part)
-                    part = jnp.concatenate([part, sums])
-                got = lax.all_gather(part, 'dp')
-                out = place_rows(got, n_own, out, base)
-                base += n_dp * n_own
-            sums = jnp.sum(got[:, n_own:n_own + 2], axis=0)
+                recv = lax.ppermute(copied, 'dp', pair)
+                if c < len(BLOCK_CALLS) - 2:
+                    recvs.append(recv)
+                    recv_firsts.append(block)
+                else:
+                    late.append((recv, block))
+                block += n_blocks
+                if c == 1:
+                    grad_scaled = grad_h * norm_vec
+                    grad_r = inv_rms * (grad_scaled - scaled_r * jnp.mean(grad_scaled * scaled_r, axis=-1, keepdims=True))
+                    grad_w = jnp.sum(grad_h * scaled_r, axis=0)
+                    own1 = own1.at[-8].set(grad_w).at[-7, 0].set(loss_part)
+                    got1 = lax.all_gather(own1, 'dp')
+
+            n_own = GRAD_CHUNKS[1]
+            n_place = PLACE_BLOCK * n_own
+            (recv, block), (last_recv, last_block) = late
+            out = place_rows(recv.reshape(-1, ROW_BLOCK, d_model), ROW_BLOCK, out, where, block, 1)
+            out = place_rows(got1, n_own, out, jnp.zeros_like(where), n_dp * GRAD_CHUNKS[0] // n_place, PLACE_BLOCK)
+            out = place_rows(last_recv.reshape(-1, ROW_BLOCK, d_model), ROW_BLOCK, out, where, last_block, 1)
+            sums = jnp.sum(got1[:, n_own:n_own + 2], axis=0)
             return sums[1, 0], grad_r.reshape(n_batch, n_seq, d_model), out, sums[0]
 
         sharded = jax.shard_map(

time: 805 us -> 604 us (0.75)
  waiting for transfers between devices: 177 us -> 16.7 us
  Pallas kernels: 562 us -> 533 us
  local copies, waits for them, and re-layouts: 17.8 us -> 9.27 us
    all_gather x2, waiting for transfers between devices: 177 us -> 0.02 us  [the longest x1 0.02 us: local_part(): got0 = lax.all_gather(own0, 'dp')]
    pallas_call x2 -> x3, Pallas kernels: 91.2 us -> 36 us  [place_rows(): pl.pallas_call(place_kernel, out_shape=jax.ShapeDtypeStruct(out.shape, ou...]
    pallas_call x4 -> x5, Pallas kernels: 295 us -> 321 us  [the longest x3 217 us: grad_rows(): pl.pallas_call(functools.partial(grad_rows_kernel, inv_n, first, n_steps,...]
    ppermute x0 -> x4, waiting for transfers between devices: none -> 16.6 us  [local_part(): recv = lax.ppermute(copied, 'dp', pair)]
  transfers between devices with their start and end apart: 8 -> 12, of which waited for: 1 -> 1; matrix products, arithmetic and copies ran while one was open for 2% -> 3% of each run, Pallas kernels for 31% -> 52%
where the time goes in v1:
time: 604 us; the launch traced here: 600 us
  Pallas kernels  533 us (88%)
  waiting for transfers between devices  16.7 us (3%)
  other arithmetic  16.3 us (3%)
  between operations  15 us (2%)
  starting transfers between devices  9.87 us (2%)
  local copies, waits for them, and re-layouts  9.27 us (2%)
    pallas_call x3, Pallas kernels, grad_rows(): pl.pallas_call(functools.partial(grad_rows_kernel, inv_n, first, n_steps,...  217 us
    pallas_call x1, Pallas kernels, exchange_tokens(): pl.pallas_call(functools.partial(exchange_kernel, plan, PIECES, SHARE_ROW...  176 us
    pallas_call x1, Pallas kernels, first_block(): pl.pallas_call(functools.partial(first_block_kernel, inv_n, first), out_s...  65.3 us
    pallas_call x1, Pallas kernels, own_rows(): pl.pallas_call(functools.partial(own_rows_kernel, inv_n, bases), out_shap...  39.4 us
    pallas_call x3, Pallas kernels, place_rows(): pl.pallas_call(place_kernel, out_shape=jax.ShapeDtypeStruct(out.shape, ou...  36 us
    ppermute x4, waiting for transfers between devices, local_part(): recv = lax.ppermute(copied, 'dp', pair)  16.6 us
  transfers between devices with their start and end apart: 12, of which 1 were waited for; matrix products, arithmetic and copies ran while one was open for 3% of the time, Pallas kernels for 52%

profile of v1, /device:TPU:0, one launch (start us, length us, event | category | flops | bytes accessed | tf_op | source)
XLA Modules:
  0.0 600.4 jit_solution(15545455464608089686)
XLA Ops:
  7.2 1.3 fusion.7
  8.7 0.7 compare_select_fusion.ids_ref
  9.4 2.5 fusion.2
  11.9 2.6 fusion.5
  14.7 0.6 pad_add_fusion.where
  15.3 176.0 %exchange_tokens.1 = (f32[2,16,264,2560]{3,2,1,0:T(8,128)}, f32[256,2560]{1,0:T(8,128)}, f32[8,256]{1,0:T(8,128)}) custom-call(bf16[256,2560]{1,0:T(8,128)(2,1)} %get-tuple-element.84.h_ref, f32[256,2560]{1,0:T(8,128)} %get-tuple-element.85.own_ref, bf16[12572,2560]{1,0:T(8,128)(2,1)} %emb_ref.9, s32[256,1]{1,0:T(8,128)} %compare_select_fusion.ids_ref, ...), custom_call_target="tpu_custom_call" | custom-call | flops 494351155200 | bytes 128737280 | tf_op jit(solution)/shard_map/exchange_tokens/pallas_call | solution.py:316
  191.3 39.4 %own_rows.1 = (f32[144,2560]{1,0:T(8,128)}, f32[104,2560]{1,0:T(8,128)}) custom-call(s32[4]{0:T(128)} %pad_add_fusion.where, bf16[12572,2560]{1,0:T(8,128)(2,1)} %emb_ref.9, bf16[12572,2560]{1,0:T(8,128)(2,1)} %emb_ref.9, f32[2,16,264,2560]{3,2,1,0:T(8,128)} %get-tuple-element.60.all_ref), custom_call_target="tpu_custom_call" | custom-call | flops 20132659200 | bytes 83886080 | tf_op jit(solution)/shard_map/own_rows/pallas_call | solution.py:388
  230.8 1.3 dynamic-slice_bitcast_fusion
  232.6 2.0 collective-permute-start.1
  234.6 1.2 collective-permute-start.2
  235.8 65.3 %first_block.1 = (f32[12572,2560]{1,0:T(8,128)}, f32[512,2560]{1,0:T(8,128)}, bf16[8192,2560]{1,0:T(8,128)(2,1)}, f32[8,8192]{1,0:T(8,128)}) custom-call(s32[4]{0:T(128)} %pad_add_fusion.where, bf16[12572,2560]{1,0:T(8,128)(2,1)} %emb_ref.9, f32[2,16,264,2560]{3,2,1,0:T(8,128)} %get-tuple-element.60.all_ref), custom_call_target="tpu_custom_call" | custom-call | flops 42949672960 | bytes 125829120 | tf_op jit(solution)/shard_map/first_block/pallas_call | solution.py:428
  301.2 1.4 subtract_reduce_fusion
  303.5 0.8 collective-permute-start.3
  304.2 1.6 collective-permute-start.4
  305.8 2.5 collective-permute-start.5
  308.4 54.8 %grad_rows.3 = (f32[12572,2560]{1,0:T(8,128)}, f32[512,2560]{1,0:T(8,128)}) custom-call(s32[4]{0:T(128)} %pad_add_fusion.where, bf16[12572,2560]{1,0:T(8,128)(2,1)} %emb_ref.9, bf16[8192,2560]{1,0:T(8,128)(2,1)} %get-tuple-element.66.h_ref, f32[8,8192]{1,0:T(8,128)} %get-tuple-element.67.stats_ref, ...), custom_call_target="tpu_custom_call", output_to_operand_aliasing={{0}: (4, {})} | custom-call | flops 42949672960 | bytes 49807360 | tf_op jit(solution)/shard_map/grad_rows/pallas_call | solution.py:550
  363.8 2.4 copy-done.1
  366.2 1.3 multiply_reduce_fusion
  367.5 1.6 scatter.6
  369.0 1.3 scatter.9
  370.4 0.5 collective-permute-start.7
  370.9 55.3 %grad_rows.4 = (f32[12572,2560]{1,0:T(8,128)}, f32[512,2560]{1,0:T(8,128)}) custom-call(s32[4]{0:T(128)} %pad_add_fusion.where, bf16[12572,2560]{1,0:T(8,128)(2,1)} %emb_ref.9, bf16[8192,2560]{1,0:T(8,128)(2,1)} %get-tuple-element.66.h_ref, f32[8,8192]{1,0:T(8,128)} %get-tuple-element.67.stats_ref, ...), custom_call_target="tpu_custom_call", output_to_operand_aliasing={{0}: (4, {})} | custom-call | flops 42949672960 | bytes 49807360 | tf_op jit(solution)/shard_map/grad_rows/pallas_call | solution.py:550
  426.3 106.6 %grad_rows.5 = (f32[12572,2560]{1,0:T(8,128)}, f32[1024,2560]{1,0:T(8,128)}) custom-call(s32[4]{0:T(128)} %pad_add_fusion.where, bf16[12572,2560]{1,0:T(8,128)(2,1)} %emb_ref.9, bf16[8192,2560]{1,0:T(8,128)(2,1)} %get-tuple-element.66.h_ref, f32[8,8192]{1,0:T(8,128)} %get-tuple-element.67.stats_ref, ...), custom_call_target="tpu_custom_call", output_to_operand_aliasing={{0}: (4, {})} | custom-call | flops 85899345920 | bytes 99614720 | tf_op jit(solution)/shard_map/grad_rows/pallas_call | solution.py:550
  533.6 3.8 fusion.1
  537.4 1.9 slice_reduce_fusion
  539.2 0.5 slice.59
  539.8 0.6 slice_reduce_fusion.1
  540.4 16.6 %collective-permute-done.9 = f32[512,2560]{1,0:T(8,128)} collective-permute-done((f32[512,2560]{1,0:T(8,128)}, f32[512,2560]{1,0:T(8,128)}, u32[]{:S(2)}, u32[]{:S(2)}) %collective-permute-start.9) | collective-permute-done | bytes 5242912 | tf_op jit(solution)/shard_map/ppermute | solution.py:659
  557.0 5.8 place_rows.3.prev_ref
  562.8 0.6 broadcast_2_where.2.where
  563.4 22.9 %place_rows.4.prev_ref = f32[12572,2560]{1,0:T(8,128)} custom-call(s32[4]{0:T(128)} %broadcast_2_where.2.where, f32[32,104,2560]{2,1,0:T(8,128)} %all-gather.4.cloned.1.call-done.src_ref, f32[12572,2560]{1,0:T(8,128)} %place_rows.3.prev_ref), custom_call_target="tpu_custom_call", output_to_operand_aliasing={{}: (2, {})} | custom-call | flops 681574400 | bytes 68157440 | tf_op jit(solution)/shard_map/place_rows/pallas_call | solution.py:578
  586.3 7.2 %place_rows.5 = f32[12572,2560]{1,0:T(8,128)} custom-call(s32[4]{0:T(128)} %pad_add_fusion.where, f32[2,512,2560]{2,1,0:T(8,128)} %bitcast.21.src_ref, f32[12572,2560]{1,0:T(8,128)} %place_rows.4.prev_ref), custom_call_target="tpu_custom_call", output_to_operand_aliasing={{}: (2, {})} | custom-call | flops 209715200 | bytes 20971520 | tf_op jit(solution)/shard_map/place_rows/pallas_call | solution.py:578
  (54 shorter events, 2.4 us)
Async XLA Ops:
  7.2 419.1 %all-gather.6.cloned.1.call-start = ((), (), s32[]{:S(2)}) async-start(), calls=%async_computation.1 | async-start | bytes 48660480 | tf_op jit(solution)/shard_map/all_gather | solution.py:643
  9.4 2.6 copy-start.5
  11.9 2.8 copy-start
  11.9 2.8 copy-start.8
  191.3 39.5 %copy-start.4 = (f32[256,2560]{1,0:T(8,128)S(1)}, f32[256,2560]{1,0:T(8,128)}, u32[]{:S(2)}) copy-start(f32[256,2560]{1,0:T(8,128)} %get-tuple-element.59) | copy-start | bytes 7864324
  230.7 306.7 %all-gather.4.cloned.1.call-start = ((), (), s32[]{:S(2)}) async-start(), calls=%async_computation | async-start | bytes 35143680 | tf_op jit(solution)/shard_map/all_gather | solution.py:671
  232.1 71.2 %collective-permute-start = (f32[64,2560]{1,0:T(8,128)}, f32[64,2560]{1,0:T(8,128)S(1)}, u32[]{:S(2)}, u32[]{:S(2)}) collective-permute-start(f32[64,2560]{1,0:T(8,128)} %get-tuple-element.90), channel_id=1, source_target_pairs={{0,32},{32,64},{64,96},{96,0},{1,33},{33,65},{65,97},{97,1},{2,34}... | collective-permute-start | bytes 1966088 | tf_op jit(solution)/shard_map/ppermute | solution.py:601
  232.6 70.7 %collective-permute-start.1 = (f32[64,2560]{1,0:T(8,128)}, f32[64,2560]{1,0:T(8,128)S(1)}, u32[]{:S(2)}, u32[]{:S(2)}) collective-permute-start(f32[64,2560]{1,0:T(8,128)} %get-tuple-element.89), channel_id=1, source_target_pairs={{0,64},{32,96},{64,0},{96,32},{1,65},{33,97},{65,1},{97,33},{2,66}... | collective-permute-start | bytes 1966088 | tf_op jit(solution)/shard_map/ppermute | solution.py:601
  234.6 66.5 %copy-start.9 = (f32[256]{0:T(256)S(1)}, f32[256]{0:T(256)}, u32[]{:S(2)}) copy-start(f32[256]{0:T(256)} %copy-done.8) | copy-start | bytes 3076
  234.6 68.7 %collective-permute-start.2 = (f32[64,2560]{1,0:T(8,128)}, f32[64,2560]{1,0:T(8,128)S(1)}, u32[]{:S(2)}, u32[]{:S(2)}) collective-permute-start(f32[64,2560]{1,0:T(8,128)} %get-tuple-element.88), channel_id=1, source_target_pairs={{0,96},{32,0},{64,32},{96,64},{1,97},{33,1},{65,33},{97,65},{2,98}... | collective-permute-start | bytes 1966088 | tf_op jit(solution)/shard_map/ppermute | solution.py:601
  303.5 59.7 %collective-permute-start.3 = (f32[64,2560]{1,0:T(8,128)S(1)}, f32[64,2560]{1,0:T(8,128)S(1)}, u32[]{:S(2)}, u32[]{:S(2)}) collective-permute-start(f32[64,2560]{1,0:T(8,128)S(1)} %add_add_fusion), channel_id=1, source_target_pairs={{0,32},{32,64},{64,96},{96,0},{1,33},{33,65},{65,97},{97,1},{2,34}... | collective-permute-start | bytes 1966088 | tf_op jit(solution)/shard_map/ppermute | solution.py:606
  304.2 59.0 %collective-permute-start.4 = (f32[64,2560]{1,0:T(8,128)S(1)}, f32[64,2560]{1,0:T(8,128)S(1)}, u32[]{:S(2)}, u32[]{:S(2)}) collective-permute-start(f32[64,2560]{1,0:T(8,128)S(1)} %add_add_fusion), channel_id=1, source_target_pairs={{0,64},{32,96},{64,0},{96,32},{1,65},{33,97},{65,1},{97,33},{2,66}... | collective-permute-start | bytes 1966088 | tf_op jit(solution)/shard_map/ppermute | solution.py:606
  305.8 57.4 %collective-permute-start.5 = (f32[64,2560]{1,0:T(8,128)S(1)}, f32[64,2560]{1,0:T(8,128)S(1)}, u32[]{:S(2)}, u32[]{:S(2)}) collective-permute-start(f32[64,2560]{1,0:T(8,128)S(1)} %add_add_fusion), channel_id=1, source_target_pairs={{0,96},{32,0},{64,32},{96,64},{1,97},{33,1},{65,33},{97,65},{2,98}... | collective-permute-start | bytes 1966088 | tf_op jit(solution)/shard_map/ppermute | solution.py:606
  363.5 2.7 copy-start.1
  363.5 2.7 copy-start.6
  363.8 3.7 copy-start.3
  370.3 55.8 %collective-permute-start.6 = (f32[512,2560]{1,0:T(8,128)}, f32[512,2560]{1,0:T(8,128)}, u32[]{:S(2)}, u32[]{:S(2)}) collective-permute-start(f32[512,2560]{1,0:T(8,128)} %get-tuple-element.77), channel_id=1, source_target_pairs={{0,1},{1,0},{2,3},{3,2},{4,5},{5,4},{6,7},{7,6},{8,9},{9,8},{10,11... | collective-permute-start | bytes 15728648 | tf_op jit(solution)/shard_map/ppermute | solution.py:659
  370.4 55.8 %collective-permute-start.7 = (f32[512,2560]{1,0:T(8,128)}, f32[512,2560]{1,0:T(8,128)}, u32[]{:S(2)}, u32[]{:S(2)}) collective-permute-start(f32[512,2560]{1,0:T(8,128)} %get-tuple-element.78), channel_id=1, source_target_pairs={{0,1},{1,0},{2,3},{3,2},{4,5},{5,4},{6,7},{7,6},{8,9},{9,8},{10,11... | collective-permute-start | bytes 15728648 | tf_op jit(solution)/shard_map/ppermute | solution.py:659
  426.2 107.2 %copy-start.11 = (f32[4,64]{1,0:T(4,128)S(1)}, f32[4,64]{1,0:T(4,128)}, u32[]{:S(2)}) copy-start(f32[4,64]{1,0:T(4,128)} %get-tuple-element.82) | copy-start | bytes 3076
  426.2 107.3 %copy-start.2 = (f32[1,256,2560]{2,1,0:T(8,128)S(1)}, f32[1,256,2560]{2,1,0:T(8,128)}, u32[]{:S(2)}) copy-start(f32[1,256,2560]{2,1,0:T(8,128)} %copy-done) | copy-start | bytes 7864324
  426.2 107.3 %copy-start.7 = (f32[2560]{0:T(1024)S(1)}, f32[2560]{0:T(1024)}, u32[]{:S(2)}) copy-start(f32[2560]{0:T(1024)} %param.13) | copy-start | bytes 30724
  426.3 107.3 %copy-start.10 = (f32[256]{0:T(256)S(1)}, f32[256]{0:T(256)}, u32[]{:S(2)}) copy-start(f32[256]{0:T(256)} %copy-done.8) | copy-start | bytes 3076
  532.9 53.4 %collective-permute-start.8 = (f32[1024,2560]{1,0:T(8,128)}, f32[1024,2560]{1,0:T(8,128)}, u32[]{:S(2)}, u32[]{:S(2)}) collective-permute-start(f32[1024,2560]{1,0:T(8,128)} %get-tuple-element.79), channel_id=1, source_target_pairs={{0,1},{1,0},{2,3},{3,2},{4,5},{5,4},{6,7},{7,6},{8,9},{9,8},{10,11... | collective-permute-start | bytes 31457288 | tf_op jit(solution)/shard_map/ppermute | solution.py:659
  533.0 24.0 %collective-permute-start.9 = (f32[512,2560]{1,0:T(8,128)}, f32[512,2560]{1,0:T(8,128)}, u32[]{:S(2)}, u32[]{:S(2)}) collective-permute-start(f32[512,2560]{1,0:T(8,128)} %get-tuple-element.80), channel_id=1, source_target_pairs={{0,1},{1,0},{2,3},{3,2},{4,5},{5,4},{6,7},{7,6},{8,9},{9,8},{10,11... | collective-permute-start | bytes 15728648 | tf_op jit(solution)/shard_map/ppermute | solution.py:659
Sparse Core Ops, SparseCore 0:
  230.8 148.3 all-gather.5
  381.5 114.0 all-gather.3

commit v2 on v1

--- a/solution.py
+++ b/solution.py
@@ -1,4 +1,5 @@
 import functools
+import itertools
 
 import jax
 import jax.numpy as jnp
@@ -10,57 +11,63 @@
 
 NORM_EPS = 1e-5
 LANES = 128
-VMEM_LIMIT = 60 * 1024 * 1024
+VMEM_LIMIT = 60 << 20
 NT = (((1,), (1,)), ((), ()))
 SHARE_ROWS = 24
-PIECES = (('share', 0, 24), ('direct', 96, 40), ('direct', 136, 40), ('direct', 176, 40), ('direct', 216, 40), ('stats', 256, 8))
+DIRECT_ROWS = 40
+PIECES = (('share', 0, SHARE_ROWS),)
+PIECES += tuple(('direct', 4 * SHARE_ROWS + i * DIRECT_ROWS, DIRECT_ROWS) for i in range(4))
+PIECES += (('stats', 0, 8),)
 PLAN = (
     ('s0,s1',),
     (),
     (),
-    ('s2,r01',),
+    ('s2',),
+    ('r01',),
     (),
     (),
     ('r11',),
-    (),
     (),
     (),
     ('r21',),
     ('s5',),
-    ('x1,r02',),
-    (),
-    (),
-    (),
-    (),
-    ('r12,f1',),
-    (),
-    (),
-    ('r22,r51,r03,r13,x2,s3,r23,r52,r04,r14,s4,r31,x3,r24', 'r53,r41,f2,x4,r32,r54,f3,f4,r42,r33,r43,r34,r44'),
+    (),
+    ('r02,x1',),
+    (),
+    (),
+    (),
+    (),
+    ('r12',),
+    (),
+    ('r22,r51,r03,x2,s3,r13,f1,r23,r52,r04,s4,r31,r14,r24', 'r53,x3,r41,f2,r32,r54,x4,f3,r42,f4,r33,r43,r34,r44'),
 )
 VOCAB_BLOCK = 1280
-GRAD_CHUNKS = (144, 96)
+GRAD_CHUNKS = (208, 64)
 ROW_BLOCK = 512
-BLOCK_CALLS = (1, 1, 1, 2)
+BLOCK_CALLS = (1, 1, 1, 1)
 TOKEN_BLOCK = 1024
 POS_BLOCK = 2
+OWN_POS_BLOCK = 4
 PLACE_BLOCK = 4
 
 
 RING = 4
-HOPS = {1: ((1, 0), (-1, 0), (0, 1), (0, -1)),
-        2: ((2, 0), (0, 2), (1, 1), (1, -1), (-1, 1), (-1, -1)),
-        3: ((1, 2), (-1, 2), (2, 1), (2, -1)),
-        4: ((2, 2),)}
+SEMS = ('plane_recv', 'x_recv', 'far_recv', 'plane_send', 'x_send', 'pair_send', 'pair_recv', 'local')
+SEMS += ('plane_send_stats', 'pair_send_stats', 'pair_recv_stats', 'local_stats')
+HOPS = {k: [hop for hop in itertools.product((0, 1, 2, -1), repeat=2) if sum(map(abs, hop)) == k] for k in range(1, 5)}
+
+SENDS = (('100201,10020-,-00201,-0020-,012210,0122-0,0-2210,0-22-0',
+          '-01210,0-1201,1001-0,01010-,1031-0,01310-'),
+         ('200201,20020-,022210,0222-0,1-1101,11010-,-12110,1131-0',
+          '--1101,-1010-,--2110,1-31-0'),
+         ('2-1101,21010-,-22110,1231-0',))
 
 
 class Exchange:
-    def __init__(self, own_ref, stats_ref, all_ref, sems, share_rows):
-        self.own_ref, self.stats_ref, self.all_ref = own_ref, stats_ref, all_ref
+    def __init__(self, own_ref, stats_ref, all_ref, all_stats_ref, sems, share_rows):
+        self.own_ref, self.stats_ref, self.all_ref, self.all_stats_ref = own_ref, stats_ref, all_ref, all_stats_ref
         self.sems = sems
-        self.n_rows = own_ref.shape[0]
         self.share_rows = share_rows
-        width = own_ref.shape[1]
-        self.quarter, self.half, self.width = width // 4, width // 2, width
         self.x = lax.axis_index('tp')
         dp = lax.axis_index('dp')
         self.core = lax.rem(dp, 2)
@@ -83,8 +90,13 @@
             start = pl.multiple_of(self.x * self.share_rows, 8)
         return pl.ds(start, size)
 
-    def block(self, hop, rows, first=0, size=None):
-        return self.all_ref.at[self.core, self.pos(hop), rows, pl.ds(first, size or self.width)]
+    def whole(self, piece):
+        return self.all_stats_ref if piece[0] == 'stats' else self.all_ref
+
+    def block(self, piece, hop, rows, first=0, size=4):
+        ref = self.whole(piece)
+        quarter = ref.shape[3] // 4
+        return ref.at[self.core, self.pos(hop), rows, pl.ds(first * quarter, size * quarter)]
 
     def send(self, src, dst, device, send, recv):
         pltpu.make_async_remote_copy(
@@ -99,64 +111,43 @@
             pl.semaphore_signal(sem, inc=1, device_id=peer, device_id_type=pl.DeviceIdType.MESH)
         pl.semaphore_wait(sem, len(peers))
 
-    def to_pair(self, src, dst):
-        self.send(src, dst, self.at(other=True), 'pair_send', self.sems['pair_recv'])
-
-    def start_own(self):
-        dst = self.all_ref.at[self.core, self.pos((0, 0)), pl.ds(0, self.n_rows)]
-        pltpu.make_async_copy(self.own_ref, dst, self.sems['local']).start()
-        self.to_pair(self.own_ref, dst)
-
-    def start_stats(self):
-        dst = self.all_ref.at[self.core, self.pos((0, 0)), pl.ds(self.n_rows, 8)]
-        pltpu.make_async_copy(self.stats_ref, dst, self.sems['local']).start()
-        self.to_pair(self.stats_ref, dst)
-
-    def plane(self, hop_src, rows, first, size, dy, dz, recv):
-        ref = self.block(hop_src, rows, first, size)
-        self.send(ref, ref, self.at(dy=dy, dz=dz), 'plane_send', recv)
+    def to_pair(self, piece, src, dst):
+        end = '_stats' if piece[0] == 'stats' else ''
+        self.send(src, dst, self.at(other=True), 'pair_send' + end, self.sems['pair_recv' + end])
+
+    def start_own(self, piece):
+        stats = piece[0] == 'stats'
+        src = self.stats_ref if stats else self.own_ref
+        dst = self.whole(piece).at[self.core, self.pos((0, 0))]
+        pltpu.make_async_copy(src, dst, self.sems['local_stats' if stats else 'local']).start()
+        self.to_pair(piece, src, dst)
 
     def round(self, p, piece, k):
         rows, recv = self.rows(piece), self.sems['plane_recv'].at[p, k - 1]
-        q, h = self.quarter, self.half
+        sent = 'plane_send_stats' if piece[0] == 'stats' else 'plane_send'
+
+        def pass_on(hop, first, size, dy, dz):
+            ref = self.block(piece, hop, rows, first, size)
+            self.send(ref, ref, self.at(dy=dy, dz=dz), sent, recv)
+
         if k == 1:
             src = self.stats_ref if piece[0] == 'stats' else self.own_ref.at[rows]
             for dy, dz in HOPS[1]:
-                self.send(src, self.block((0, 0), rows), self.at(dy=dy, dz=dz), 'plane_send', recv)
-        elif k == 2:
-            for s in (1, -1):
-                for o in (1, -1):
-                    self.plane((o, 0), rows, 0, h, 0, s, recv)
-                    self.plane((0, o), rows, h, h, s, 0, recv)
-            self.plane((-1, 0), rows, q, h, 1, 0, recv)
-            self.plane((0, -1), rows, q, h, 0, 1, recv)
-            for first in (0, 3 * q):
-                self.plane((1, 0), rows, first, q, -1, 0, recv)
-                self.plane((0, 1), rows, first, q, 0, -1, recv)
-        elif k == 3:
-            for s in (1, -1):
-                self.plane((2, 0), rows, 0, h, 0, s, recv)
-                self.plane((0, 2), rows, h, h, s, 0, recv)
-            for o in (1, -1):
-                self.plane((o, -1), rows, q, q, 0, 1, recv)
-                self.plane((o, 1), rows, 0, q, 0, -1, recv)
-                self.plane((-1, o), rows, h, q, 1, 0, recv)
-                self.plane((1, o), rows, 3 * q, q, -1, 0, recv)
+                self.send(src, self.block(piece, (0, 0), rows), self.at(dy=dy, dz=dz), sent, recv)
         else:
-            self.plane((2, -1), rows, q, q, 0, 1, recv)
-            self.plane((2, 1), rows, 0, q, 0, -1, recv)
-            self.plane((-1, 2), rows, h, q, 1, 0, recv)
-            self.plane((1, 2), rows, 3 * q, q, -1, 0, recv)
+            for code in ','.join(SENDS[k - 2]).split(','):
+                y, z, first, size, dy, dz = ['-0123'.index(c) - 1 for c in code]
+                pass_on((y, z), first, size, dy, dz)
 
     def wait(self, ref, sem):
         pltpu.make_async_copy(ref, ref, sem).wait()
 
     def finish_round(self, p, piece, k):
         n, rows = len(HOPS[k]), self.rows(piece)
-        self.wait(self.all_ref.at[0, pl.ds(0, n), pl.ds(0, piece[2])], self.sems['plane_recv'].at[p, k - 1])
+        self.wait(self.whole(piece).at[0, pl.ds(0, n), pl.ds(0, piece[2])], self.sems['plane_recv'].at[p, k - 1])
         for hop in HOPS[k]:
-            ref = self.block(hop, rows)
-            self.to_pair(ref, ref)
+            ref = self.block(piece, hop, rows)
+            self.to_pair(piece, ref, ref)
             if piece[0] == 'share':
                 for s in (1, -1):
                     self.send(ref, ref, self.at(dx=s), 'x_send', self.sems['x_recv'].at[k - 1])
@@ -166,41 +157,41 @@
         return pl.ds(pl.multiple_of(x * self.share_rows, 8), self.share_rows)
 
     def along_x(self, k):
-        n = len(HOPS[k])
+        n, share = len(HOPS[k]), PIECES[0]
         self.wait(self.all_ref.at[0, pl.ds(0, n), pl.ds(0, 2 * self.share_rows)], self.sems['x_recv'].at[k - 1])
         for hop in HOPS[k]:
-            for dx, first in ((-1, 0), (1, self.half)):
+            for dx, first in ((-1, 0), (1, 2)):
                 rows = self.share_of(dx)
-                ref = self.block(hop, rows, first, self.half)
+                ref = self.block(share, hop, rows, first, 2)
                 self.send(ref, ref, self.at(dx=-dx), 'x_send', self.sems['far_recv'].at[k - 1])
-                ref = self.block(hop, rows)
-                self.to_pair(ref, ref)
+                ref = self.block(share, hop, rows)
+                self.to_pair(share, ref, ref)
 
     def finish_x(self, k):
-        n, rows = len(HOPS[k]), self.share_of(2)
+        n, share, rows = len(HOPS[k]), PIECES[0], self.share_of(2)
         self.wait(self.all_ref.at[0, pl.ds(0, n), pl.ds(0, self.share_rows)], self.sems['far_recv'].at[k - 1])
         for hop in HOPS[k]:
-            ref = self.block(hop, rows)
-            self.to_pair(ref, ref)
+            ref = self.block(share, hop, rows)
+            self.to_pair(share, ref, ref)
 
     def finish(self, pieces):
-        n_other = RING * RING - 1
-        total = sum(size for _, _, size in pieces)
-        self.wait(self.all_ref.at[0], self.sems['pair_recv'])
-        self.wait(self.all_ref.at[0], self.sems['pair_send'])
-        self.wait(self.all_ref.at[0, pl.ds(0, n_other), pl.ds(0, total)], self.sems['plane_send'])
-        self.wait(self.all_ref.at[0, pl.ds(0, n_other), pl.ds(0, 3 * self.share_rows)], self.sems['x_send'])
-        self.wait(self.all_ref.at[0, 0], self.sems['local'])
+        others = pl.ds(0, RING * RING - 1)
+        total = sum(size for kind, _, size in pieces if kind != 'stats')
+        for end, ref in (('', self.all_ref), ('_stats', self.all_stats_ref)):
+            self.wait(ref.at[0], self.sems['pair_recv' + end])
+            self.wait(ref.at[0], self.sems['pair_send' + end])
+            self.wait(ref.at[0, 0], self.sems['local' + end])
+        self.wait(self.all_ref.at[0, others, pl.ds(0, total)], self.sems['plane_send'])
+        self.wait(self.all_stats_ref.at[0, others], self.sems['plane_send_stats'])
+        self.wait(self.all_ref.at[0, others, pl.ds(0, 3 * self.share_rows)], self.sems['x_send'])
 
 
 def exchange_kernel(plan, pieces, share_rows, vocab, inv_n, h_ref, own_ref, emb_ref, ids_ref, tgt_ref,
-                    all_ref, grad_ref, stats_out_ref, logits_ref, m_ref, s_ref, t_ref, col_ref, stats_ref, part_ref,
-                    plane_recv, x_recv, far_recv, pair_recv, plane_send, x_send, pair_send, local, part_recv, part_send):
+                    all_ref, all_stats_ref, grad_ref, stats_out_ref,
+                    logits_ref, m_ref, s_ref, t_ref, col_ref, stats_ref, part_ref, part_recv, part_send, *sem_refs):
     step = pl.program_id(0)
     n_tiles, rows, width = logits_ref.shape
-    sems = dict(plane_recv=plane_recv, x_recv=x_recv, far_recv=far_recv, pair_recv=pair_recv, plane_send=plane_send,
-                x_send=x_send, pair_send=pair_send, local=local)
-    ex = Exchange(own_ref, stats_ref, all_ref, sems, share_rows)
+    ex = Exchange(own_ref, stats_ref, all_ref, all_stats_ref, dict(zip(SEMS, sem_refs)), share_rows)
 
     def run(event):
         kind, *nums = event
@@ -224,7 +215,7 @@
             def _(i=i, events=events):
                 if i == 0:
                     ex.barrier()
-                    ex.start_own()
+                    ex.start_own(pieces[0])
                 for event in events:
                     run(event)
                 if i == len(plan) - 1:
@@ -286,19 +277,26 @@
         stats_ref[...] = jnp.zeros_like(stats_ref)
         stats_ref[:, :rows] = final
         col_ref[...] = jnp.concatenate([final, jnp.zeros((LANES - 8, rows), jnp.float32)]).T
-        ex.start_stats()
+        ex.start_own(pieces[-1])
 
     def add_grad(masked):
         tile = step - n_tiles
         ids = lax.broadcasted_iota(jnp.int32, (rows, width), 1) + tile * width
         grad = jnp.exp(logits_ref[tile] - col_ref[:, 0:1]) * col_ref[:, 1:2]
         grad -= jnp.where(ids == ids_ref[...], inv_n, 0.0)
-        emb = emb_ref[...]
         if masked:
             grad = jnp.where(ids < vocab, grad, 0.0)
-            emb_ids = lax.broadcasted_iota(jnp.int32, emb.shape, 0) + tile * width
-            emb = jnp.where(emb_ids < vocab, emb.astype(jnp.float32), 0.0).astype(emb.dtype)
-        grad_ref[...] += jnp.dot(grad.astype(jnp.bfloat16), emb, preferred_element_type=jnp.float32)
+        grad = grad.astype(jnp.bfloat16)
+        n_cols = grad_ref.shape[1] // 4
+
+        @pl.loop(0, 4)
+        def _(j):
+            cols = pl.ds(pl.multiple_of(j * n_cols, LANES), n_cols)
+            emb = emb_ref[:, cols]
+            if masked:
+                emb_ids = lax.broadcasted_iota(jnp.int32, emb.shape, 0) + tile * width
+                emb = jnp.where(emb_ids < vocab, emb.astype(jnp.float32), 0.0).astype(emb.dtype)
+            grad_ref[:, cols] += jnp.dot(grad, emb, preferred_element_type=jnp.float32)
 
     pl.when(jnp.logical_and(step >= n_tiles, step < 2 * n_tiles - 1))(lambda: add_grad(False))
     pl.when(step == 2 * n_tiles - 1)(lambda: add_grad(True))
@@ -315,16 +313,17 @@
     whole = pl.BlockSpec(memory_space=pltpu.VMEM)
     return pl.pallas_call(
         functools.partial(exchange_kernel, plan, PIECES, SHARE_ROWS, vocab, inv_n),
-        out_shape=(jax.ShapeDtypeStruct((2, n_dp // 2, rows + 8, width), jnp.float32),
+        out_shape=(jax.ShapeDtypeStruct((2, n_dp // 2, rows, width), jnp.float32),
+                   jax.ShapeDtypeStruct((2, n_dp // 2, 8, 4 * LANES), jnp.float32),
                    jax.ShapeDtypeStruct((rows, width), jnp.float32),
                    jax.ShapeDtypeStruct((8, rows), jnp.float32)),
         grid=(n_steps,),
         in_specs=[whole, whole, pl.BlockSpec((VOCAB_BLOCK, width), emb_tile), whole, whole],
-        out_specs=(pl.BlockSpec(memory_space=pl.ANY), whole, whole),
+        out_specs=(pl.BlockSpec(memory_space=pl.ANY), pl.BlockSpec(memory_space=pl.ANY), whole, whole),
         scratch_shapes=[pltpu.VMEM((n_tiles, rows, VOCAB_BLOCK), jnp.float32)]
                        + [pltpu.VMEM((rows, LANES), jnp.float32)] * 4
-                       + [pltpu.VMEM((8, width), jnp.float32), pltpu.VMEM((RING, 8, rows), jnp.float32)]
-                       + [dma((len(PIECES), 4)), dma((4,)), dma((4,))] + [dma] * 7,
+                       + [pltpu.VMEM((8, 4 * LANES), jnp.float32), pltpu.VMEM((RING, 8, rows), jnp.float32)]
+                       + [dma, dma, dma((len(PIECES), 4)), dma((4,)), dma((4,))] + [dma] * (len(SEMS) - 3),
         compiler_params=pltpu.CompilerParams(
             vmem_limit_bytes=VMEM_LIMIT, collective_id=0, has_side_effects=True),
         cost_estimate=pl.CostEstimate(
@@ -344,19 +343,19 @@
     return (lax.broadcasted_iota(jnp.int32, (n_rows, 1), 0) + first).astype(jnp.float32)
 
 
-def load_tokens(all_ref):
-    blocks, rows = all_ref.shape[1], all_ref.shape[2] - 8
-    h_blk = all_ref[0, :, :rows, :].reshape(blocks * rows, all_ref.shape[3]).astype(jnp.bfloat16)
-    return h_blk, jnp.concatenate([all_ref[0, i, rows:, :rows] for i in range(blocks)], axis=1)
-
-
-def token_spec(gathered):
-    _, n_pos, n_in, width = gathered.shape
-    per_core = n_pos // POS_BLOCK
-    return pl.BlockSpec((1, POS_BLOCK, n_in, width), lambda i, where: (i // per_core, lax.rem(i, per_core), 0, 0))
-
-
-def own_rows_kernel(inv_n, bases, where, emb0_ref, emb1_ref, all_ref, own0_ref, own1_ref, emb_ref, acc_ref):
+def load_tokens(all_ref, all_stats_ref):
+    _, blocks, rows, width = all_ref.shape
+    h_blk = all_ref[0].reshape(blocks * rows, width).astype(jnp.bfloat16)
+    return h_blk, jnp.concatenate([all_stats_ref[0, i, :, :rows] for i in range(blocks)], axis=1)
+
+
+def token_specs(gathered, pos_block):
+    return [pl.BlockSpec((1, pos_block) + arr.shape[2:],
+                         lambda i, where: (i * pos_block // arr.shape[1], lax.rem(i, arr.shape[1] // pos_block), 0, 0))
+            for arr in gathered]
+
+
+def own_rows_kernel(inv_n, bases, where, emb0_ref, emb1_ref, all_ref, all_stats_ref, own0_ref, own1_ref, emb_ref, acc_ref):
     n0, n1 = emb0_ref.shape[0], emb1_ref.shape[0]
 
     @pl.when(pl.program_id(0) == 0)
@@ -368,7 +367,7 @@
     first0, first1 = [where[1] + base + where[0] * n for base, n in zip(bases, (n0, n1))]
     row = lax.broadcasted_iota(jnp.int32, (n0 + n1, 1), 0)
     row_ids = (row + jnp.where(row < n0, first0, first1 - n0)).astype(jnp.float32)
-    h_blk, stats = load_tokens(all_ref)
+    h_blk, stats = load_tokens(all_ref, all_stats_ref)
     acc_ref[...] += row_grads(inv_n, emb_ref[...], row_ids, h_blk, stats)
 
     @pl.when(pl.program_id(0) == pl.num_programs(0) - 1)
@@ -380,7 +379,7 @@
 
 def own_rows(emb, gathered, where, inv_n, n_dp):
     width = emb.shape[1]
-    n_tok = gathered.shape[0] * gathered.shape[1] * (gathered.shape[2] - 8)
+    n_tok = gathered[0].size // width
     n0, n1 = GRAD_CHUNKS
     bases = (0, n_dp * n0)
     emb_spec = lambda base, n: pl.BlockSpec((n, width), lambda i, where: (base // n + where[0], 0))
@@ -390,25 +389,25 @@
         out_shape=(jax.ShapeDtypeStruct((n0, width), jnp.float32), jax.ShapeDtypeStruct((n1 + 8, width), jnp.float32)),
         grid_spec=pltpu.PrefetchScalarGridSpec(
             num_scalar_prefetch=1,
-            grid=(gathered.shape[0] * gathered.shape[1] // POS_BLOCK,),
-            in_specs=[emb_spec(bases[0], n0), emb_spec(bases[1], n1), token_spec(gathered)],
+            grid=(gathered[0].shape[0] * gathered[0].shape[1] // OWN_POS_BLOCK,),
+            in_specs=[emb_spec(bases[0], n0), emb_spec(bases[1], n1)] + token_specs(gathered, OWN_POS_BLOCK),
             out_specs=(whole(n0), whole(n1 + 8)),
             scratch_shapes=[pltpu.VMEM((n0 + n1, width), jnp.bfloat16), pltpu.VMEM((n0 + n1, width), jnp.float32)]),
         compiler_params=pltpu.CompilerParams(vmem_limit_bytes=VMEM_LIMIT),
         cost_estimate=pl.CostEstimate(
             flops=4 * (n0 + n1) * n_tok * width, bytes_accessed=n_tok * width * 4, transcendentals=(n0 + n1) * n_tok),
         name="own_rows",
-    )(where, emb, emb, gathered)
-
-
-def first_block_kernel(inv_n, first, where, emb_ref, all_ref, out_ref, copy_ref, h_ref, stats_ref):
+    )(where, emb, emb, *gathered)
+
+
+def first_block_kernel(inv_n, first, where, emb_ref, all_ref, all_stats_ref, out_ref, copy_ref, h_ref, stats_ref):
     step, last = pl.program_id(0), pl.num_programs(0) - 1
 
     @pl.when(step == 0)
     def _():
         out_ref[...] = jnp.zeros_like(out_ref)
 
-    h_blk, stats = load_tokens(all_ref)
+    h_blk, stats = load_tokens(all_ref, all_stats_ref)
     h_ref[...] = h_blk
     stats_ref[...] = stats
     n_rows = emb_ref.shape[0]
@@ -422,8 +421,8 @@
 
 def first_block(emb, gathered, where, inv_n, first):
     vocab, width = emb.shape
-    n_tok = gathered.shape[0] * gathered.shape[1] * (gathered.shape[2] - 8)
-    per_step = POS_BLOCK * (gathered.shape[2] - 8)
+    n_tok = gathered[0].size // width
+    per_step = POS_BLOCK * gathered[0].shape[2]
     row_spec = pl.BlockSpec((ROW_BLOCK, width), lambda i, where: (first + where[2], 0))
     return pl.pallas_call(
         functools.partial(first_block_kernel, inv_n, first),
@@ -434,7 +433,7 @@
         grid_spec=pltpu.PrefetchScalarGridSpec(
             num_scalar_prefetch=1,
             grid=(n_tok // per_step,),
-            in_specs=[row_spec, token_spec(gathered)],
+            in_specs=[row_spec] + token_specs(gathered, POS_BLOCK),
             out_specs=(row_spec, pl.BlockSpec((ROW_BLOCK, width), lambda i, where: (0, 0)),
                        pl.BlockSpec((per_step, width), lambda i, where: (i, 0)),
                        pl.BlockSpec((8, per_step), lambda i, where: (0, i)))),
@@ -442,7 +441,7 @@
         cost_estimate=pl.CostEstimate(
             flops=4 * ROW_BLOCK * n_tok * width, bytes_accessed=n_tok * width * 6, transcendentals=ROW_BLOCK * n_tok),
         name="first_block",
-    )(where, emb, gathered)
+    )(where, emb, *gathered)
 
 
 class Placing:
@@ -633,7 +632,7 @@
             local_ids = (tgt_rows - tp_idx * vocab_loc)[:, None]
             local_ids = jnp.where(local_ids < vocab_loc, local_ids, -1)
             tgt_row = tgt_rows.astype(jnp.float32)[None]
-            gathered, grad_h, stats = exchange_tokens(h_act, h_wide, emb_loc, local_ids, tgt_row, inv_n, n_dp)
+            *gathered, grad_h, stats = exchange_tokens(h_act, h_wide, emb_loc, local_ids, tgt_row, inv_n, n_dp)
             loss_part = jnp.sum(stats[0] + jnp.log(stats[3]) - stats[4]) * inv_n
 
             per_core = sum(BLOCK_CALLS)

time: 604 us -> 558 us (0.924)
  Pallas kernels: 533 us -> 485 us
    pallas_call x3, Pallas kernels: 217 us -> 184 us  [grad_rows(): pl.pallas_call(functools.partial(grad_rows_kernel, inv_n, first, n_steps,...]
    ppermute x4, waiting for transfers between devices: 16.6 us -> 0.01 us  [local_part(): recv = lax.ppermute(copied, 'dp', pair)]
    all_gather x1, waiting for transfers between devices: 0.01 us -> 10.7 us  [local_part(): got1 = lax.all_gather(own1, 'dp')]
    all_gather x1, waiting for transfers between devices: 0.02 us -> 8.6 us  [local_part(): got0 = lax.all_gather(own0, 'dp')]
    pallas_call x3, Pallas kernels: 36 us -> 28.1 us  [place_rows(): pl.pallas_call(place_kernel, out_shape=jax.ShapeDtypeStruct(out.shape, ou...]
  transfers between devices with their start and end apart: 12 -> 12, of which waited for: 1 -> 2; matrix products, arithmetic and copies ran while one was open for 3% -> 3% of each run, Pallas kernels for 52% -> 49%
where the time goes in v2:
time: 558 us; the launch traced here: 555 us
  Pallas kernels  485 us (87%)
  waiting for transfers between devices  19.4 us (3%)
  other arithmetic  16.4 us (3%)
  between operations  15 us (3%)
  starting transfers between devices  10.5 us (2%)
  local copies, waits for them, and re-layouts  9.27 us (2%)
    pallas_call x3, Pallas kernels, grad_rows(): pl.pallas_call(functools.partial(grad_rows_kernel, inv_n, first, n_steps,...  184 us
    pallas_call x1, Pallas kernels, exchange_tokens(): pl.pallas_call(functools.partial(exchange_kernel, plan, PIECES, SHARE_ROW...  172 us
    pallas_call x1, Pallas kernels, first_block(): pl.pallas_call(functools.partial(first_block_kernel, inv_n, first), out_s...  64.3 us
    pallas_call x1, Pallas kernels, own_rows(): pl.pallas_call(functools.partial(own_rows_kernel, inv_n, bases), out_shap...  35.6 us
    pallas_call x3, Pallas kernels, place_rows(): pl.pallas_call(place_kernel, out_shape=jax.ShapeDtypeStruct(out.shape, ou...  28.1 us
  transfers between devices with their start and end apart: 12, of which 2 were waited for; matrix products, arithmetic and copies ran while one was open for 3% of the time, Pallas kernels for 49%

profile of v2, /device:TPU:0, one launch (start us, length us, event | category | flops | bytes accessed | tf_op | source)
XLA Modules:
  0.0 555.3 jit_solution(15375110697257169102)
XLA Ops:
  7.2 1.3 fusion.7
  8.7 0.7 compare_select_fusion.ids_ref
  9.4 2.5 fusion.2
  11.9 2.7 fusion.5
  14.7 0.7 pad_add_fusion.where
  15.4 172.3 %exchange_tokens.1 = (f32[2,16,256,2560]{3,2,1,0:T(8,128)}, f32[2,16,8,512]{3,2,1,0:T(8,128)}, f32[256,2560]{1,0:T(8,128)}, f32[8,256]{1,0:T(8,128)}) custom-call(bf16[256,2560]{1,0:T(8,128)(2,1)} %get-tuple-element.88.h_ref, f32[256,2560]{1,0:T(8,128)} %get-tuple-element.89.own_ref, bf16[12572,2560]{1,0:T(8,128)(2,1)} %emb_ref.9, ...), custom_call_target="tpu_custom_call" | custom-call | flops 494351155200 | bytes 128737280 | tf_op jit(solution)/shard_map/exchange_tokens/pallas_call | solution.py:314
  187.6 35.6 %own_rows.1 = (f32[208,2560]{1,0:T(8,128)}, f32[72,2560]{1,0:T(8,128)}) custom-call(s32[4]{0:T(128)} %pad_add_fusion.where, bf16[12572,2560]{1,0:T(8,128)(2,1)} %emb_ref.9, bf16[12572,2560]{1,0:T(8,128)(2,1)} %emb_ref.9, f32[2,16,256,2560]{3,2,1,0:T(8,128)} %get-tuple-element.63.all_ref, f32[2,16,8,512]{3,2,1,0:T(8,128)} %get-tuple-element.64.all_stats_ref), custom_call_target="tpu_custom_call" | custom-call | flops 22817013760 | bytes 83886080 | tf_op jit(solution)/shard_map/own_rows/pallas_call | solution.py:387
  223.6 1.3 dynamic-slice_bitcast_fusion
  225.4 2.0 collective-permute-start.1
  227.4 1.7 collective-permute-start.2
  229.1 64.3 %first_block.1 = (f32[12572,2560]{1,0:T(8,128)}, f32[512,2560]{1,0:T(8,128)}, bf16[8192,2560]{1,0:T(8,128)(2,1)}, f32[8,8192]{1,0:T(8,128)}) custom-call(s32[4]{0:T(128)} %pad_add_fusion.where, bf16[12572,2560]{1,0:T(8,128)(2,1)} %emb_ref.9, f32[2,16,256,2560]{3,2,1,0:T(8,128)} %get-tuple-element.63.all_ref, f32[2,16,8,512]{3,2,1,0:T(8,128)} %get-tuple-element.64.all_stats_ref), custom_call_target="tpu_custom_call" | custom-call | flops 42949672960 | bytes 125829120 | tf_op jit(solution)/shard_map/first_block/pallas_call | solution.py:427
  293.5 1.4 subtract_reduce_fusion
  295.8 0.8 collective-permute-start.3
  296.6 1.8 collective-permute-start.4
  298.3 2.5 collective-permute-start.5
  300.9 54.9 %grad_rows.3 = (f32[12572,2560]{1,0:T(8,128)}, f32[512,2560]{1,0:T(8,128)}) custom-call(s32[4]{0:T(128)} %pad_add_fusion.where, bf16[12572,2560]{1,0:T(8,128)(2,1)} %emb_ref.9, bf16[8192,2560]{1,0:T(8,128)(2,1)} %get-tuple-element.70.h_ref, f32[8,8192]{1,0:T(8,128)} %get-tuple-element.71.stats_ref, ...), custom_call_target="tpu_custom_call", output_to_operand_aliasing={{0}: (4, {})} | custom-call | flops 42949672960 | bytes 49807360 | tf_op jit(solution)/shard_map/grad_rows/pallas_call | solution.py:549
  356.4 2.5 copy-done.1
  358.9 1.3 multiply_reduce_fusion
  360.1 1.6 scatter.6
  361.7 1.3 scatter.9
  363.6 54.8 %grad_rows.4 = (f32[12572,2560]{1,0:T(8,128)}, f32[512,2560]{1,0:T(8,128)}) custom-call(s32[4]{0:T(128)} %pad_add_fusion.where, bf16[12572,2560]{1,0:T(8,128)(2,1)} %emb_ref.9, bf16[8192,2560]{1,0:T(8,128)(2,1)} %get-tuple-element.70.h_ref, f32[8,8192]{1,0:T(8,128)} %get-tuple-element.71.stats_ref, ...), custom_call_target="tpu_custom_call", output_to_operand_aliasing={{0}: (4, {})} | custom-call | flops 42949672960 | bytes 49807360 | tf_op jit(solution)/shard_map/grad_rows/pallas_call | solution.py:549
  418.7 8.6 %all-gather.6.cloned.1.call-done = f32[6656,2560]{1,0:T(8,128)} async-done(((f32[208,2560]{1,0:T(8,128)}), f32[6656,2560]{1,0:T(8,128)}) %all-gather.6.cloned.1.call-update) | async-done | bytes 68157456 | tf_op jit(solution)/shard_map/all_gather | solution.py:642
  427.3 74.7 %grad_rows.5 = (f32[12572,2560]{1,0:T(8,128)}, f32[512,2560]{1,0:T(8,128)}) custom-call(s32[4]{0:T(128)} %pad_add_fusion.where, bf16[12572,2560]{1,0:T(8,128)(2,1)} %emb_ref.9, bf16[8192,2560]{1,0:T(8,128)(2,1)} %get-tuple-element.70.h_ref, f32[8,8192]{1,0:T(8,128)} %get-tuple-element.71.stats_ref, ...), custom_call_target="tpu_custom_call", output_to_operand_aliasing={{0}: (4, {})} | custom-call | flops 42949672960 | bytes 49807360 | tf_op jit(solution)/shard_map/grad_rows/pallas_call | solution.py:549
  502.2 3.8 fusion.1
  506.0 10.7 %all-gather.4.cloned.1.call-done.src_ref = f32[32,72,2560]{2,1,0:T(8,128)} async-done(((f32[1,72,2560]{2,1,0:T(8,128)}), f32[32,72,2560]{2,1,0:T(8,128)}) %all-gather.4.cloned.1.call-update) | async-done | bytes 23592976 | tf_op jit(solution)/shard_map/all_gather | solution.py:670
  516.7 1.9 slice_reduce_fusion
  518.6 0.5 slice.59
  519.1 0.6 slice_reduce_fusion.1
  519.7 5.8 %place_rows.3.prev_ref = f32[12572,2560]{1,0:T(8,128)} custom-call(s32[4]{0:T(128)} %pad_add_fusion.where, f32[1,512,2560]{2,1,0:T(8,128)} %bitcast.22.src_ref, f32[12572,2560]{1,0:T(8,128)} %get-tuple-element.85.prev_ref), custom_call_target="tpu_custom_call", output_to_operand_aliasing={{}: (2, {})} | custom-call | flops 104857600 | bytes 10485760 | tf_op jit(solution)/shard_map/place_rows/pallas_call | solution.py:577
  525.6 0.6 broadcast_2_where.2.where
  526.2 17.2 %place_rows.4.prev_ref = f32[12572,2560]{1,0:T(8,128)} custom-call(s32[4]{0:T(128)} %broadcast_2_where.2.where, f32[32,72,2560]{2,1,0:T(8,128)} %all-gather.4.cloned.1.call-done.src_ref, f32[12572,2560]{1,0:T(8,128)} %place_rows.3.prev_ref), custom_call_target="tpu_custom_call", output_to_operand_aliasing={{}: (2, {})} | custom-call | flops 471859200 | bytes 47185920 | tf_op jit(solution)/shard_map/place_rows/pallas_call | solution.py:577
  543.4 5.1 place_rows.5
  (54 shorter events, 2.8 us)
Async XLA Ops:
  7.2 420.1 %all-gather.6.cloned.1.call-start = ((), (), s32[]{:S(2)}) async-start(), calls=%async_computation.1 | async-start | bytes 70287360 | tf_op jit(solution)/shard_map/all_gather | solution.py:642
  9.4 2.6 copy-start.5
  11.9 2.8 copy-start
  11.9 2.8 copy-start.8
  187.6 36.0 %copy-start.4 = (f32[256,2560]{1,0:T(8,128)S(1)}, f32[256,2560]{1,0:T(8,128)}, u32[]{:S(2)}) copy-start(f32[256,2560]{1,0:T(8,128)} %get-tuple-element.62) | copy-start | bytes 7864324
  223.3 293.4 %all-gather.4.cloned.1.call-start = ((), (), s32[]{:S(2)}) async-start(), calls=%async_computation | async-start | bytes 24330240 | tf_op jit(solution)/shard_map/all_gather | solution.py:670
  225.0 70.6 %collective-permute-start = (f32[64,2560]{1,0:T(8,128)}, f32[64,2560]{1,0:T(8,128)S(1)}, u32[]{:S(2)}, u32[]{:S(2)}) collective-permute-start(f32[64,2560]{1,0:T(8,128)} %get-tuple-element.94), channel_id=1, source_target_pairs={{0,32},{32,64},{64,96},{96,0},{1,33},{33,65},{65,97},{97,1},{2,34}... | collective-permute-start | bytes 1966088 | tf_op jit(solution)/shard_map/ppermute | solution.py:600
  225.4 70.2 %collective-permute-start.1 = (f32[64,2560]{1,0:T(8,128)}, f32[64,2560]{1,0:T(8,128)S(1)}, u32[]{:S(2)}, u32[]{:S(2)}) collective-permute-start(f32[64,2560]{1,0:T(8,128)} %get-tuple-element.93), channel_id=1, source_target_pairs={{0,64},{32,96},{64,0},{96,32},{1,65},{33,97},{65,1},{97,33},{2,66}... | collective-permute-start | bytes 1966088 | tf_op jit(solution)/shard_map/ppermute | solution.py:600
  227.4 66.0 %copy-start.9 = (f32[256]{0:T(256)S(1)}, f32[256]{0:T(256)}, u32[]{:S(2)}) copy-start(f32[256]{0:T(256)} %copy-done.8) | copy-start | bytes 3076
  227.4 68.2 %collective-permute-start.2 = (f32[64,2560]{1,0:T(8,128)}, f32[64,2560]{1,0:T(8,128)S(1)}, u32[]{:S(2)}, u32[]{:S(2)}) collective-permute-start(f32[64,2560]{1,0:T(8,128)} %get-tuple-element.92), channel_id=1, source_target_pairs={{0,96},{32,0},{64,32},{96,64},{1,97},{33,1},{65,33},{97,65},{2,98}... | collective-permute-start | bytes 1966088 | tf_op jit(solution)/shard_map/ppermute | solution.py:600
  295.8 60.0 %collective-permute-start.3 = (f32[64,2560]{1,0:T(8,128)S(1)}, f32[64,2560]{1,0:T(8,128)S(1)}, u32[]{:S(2)}, u32[]{:S(2)}) collective-permute-start(f32[64,2560]{1,0:T(8,128)S(1)} %add_add_fusion), channel_id=1, source_target_pairs={{0,32},{32,64},{64,96},{96,0},{1,33},{33,65},{65,97},{97,1},{2,34}... | collective-permute-start | bytes 1966088 | tf_op jit(solution)/shard_map/ppermute | solution.py:605
  296.6 59.2 %collective-permute-start.4 = (f32[64,2560]{1,0:T(8,128)S(1)}, f32[64,2560]{1,0:T(8,128)S(1)}, u32[]{:S(2)}, u32[]{:S(2)}) collective-permute-start(f32[64,2560]{1,0:T(8,128)S(1)} %add_add_fusion), channel_id=1, source_target_pairs={{0,64},{32,96},{64,0},{96,32},{1,65},{33,97},{65,1},{97,33},{2,66}... | collective-permute-start | bytes 1966088 | tf_op jit(solution)/shard_map/ppermute | solution.py:605
  298.3 57.5 %collective-permute-start.5 = (f32[64,2560]{1,0:T(8,128)S(1)}, f32[64,2560]{1,0:T(8,128)S(1)}, u32[]{:S(2)}, u32[]{:S(2)}) collective-permute-start(f32[64,2560]{1,0:T(8,128)S(1)} %add_add_fusion), channel_id=1, source_target_pairs={{0,96},{32,0},{64,32},{96,64},{1,97},{33,1},{65,33},{97,65},{2,98}... | collective-permute-start | bytes 1966088 | tf_op jit(solution)/shard_map/ppermute | solution.py:605
  356.1 2.7 copy-start.1
  356.1 2.7 copy-start.6
  356.4 3.8 copy-start.3
  363.0 55.7 %collective-permute-start.6 = (f32[512,2560]{1,0:T(8,128)}, f32[512,2560]{1,0:T(8,128)}, u32[]{:S(2)}, u32[]{:S(2)}) collective-permute-start(f32[512,2560]{1,0:T(8,128)} %get-tuple-element.81), channel_id=1, source_target_pairs={{0,1},{1,0},{2,3},{3,2},{4,5},{5,4},{6,7},{7,6},{8,9},{9,8},{10,11... | collective-permute-start | bytes 15728648 | tf_op jit(solution)/shard_map/ppermute | solution.py:658
  363.1 55.6 %collective-permute-start.7 = (f32[512,2560]{1,0:T(8,128)}, f32[512,2560]{1,0:T(8,128)}, u32[]{:S(2)}, u32[]{:S(2)}) collective-permute-start(f32[512,2560]{1,0:T(8,128)} %get-tuple-element.82), channel_id=1, source_target_pairs={{0,1},{1,0},{2,3},{3,2},{4,5},{5,4},{6,7},{7,6},{8,9},{9,8},{10,11... | collective-permute-start | bytes 15728648 | tf_op jit(solution)/shard_map/ppermute | solution.py:658
  418.4 101.4 %collective-permute-start.9 = (f32[512,2560]{1,0:T(8,128)}, f32[512,2560]{1,0:T(8,128)}, u32[]{:S(2)}, u32[]{:S(2)}) collective-permute-start(f32[512,2560]{1,0:T(8,128)} %get-tuple-element.84), channel_id=1, source_target_pairs={{0,1},{1,0},{2,3},{3,2},{4,5},{5,4},{6,7},{7,6},{8,9},{9,8},{10,11... | collective-permute-start | bytes 15728648 | tf_op jit(solution)/shard_map/ppermute | solution.py:658
  427.3 74.8 %copy-start.11 = (f32[4,64]{1,0:T(4,128)S(1)}, f32[4,64]{1,0:T(4,128)}, u32[]{:S(2)}) copy-start(f32[4,64]{1,0:T(4,128)} %get-tuple-element.86) | copy-start | bytes 3076
  427.3 74.9 %copy-start.2 = (f32[1,256,2560]{2,1,0:T(8,128)S(1)}, f32[1,256,2560]{2,1,0:T(8,128)}, u32[]{:S(2)}) copy-start(f32[1,256,2560]{2,1,0:T(8,128)} %copy-done) | copy-start | bytes 7864324
  427.3 74.9 %copy-start.7 = (f32[2560]{0:T(1024)S(1)}, f32[2560]{0:T(1024)}, u32[]{:S(2)}) copy-start(f32[2560]{0:T(1024)} %param.13) | copy-start | bytes 30724
  427.3 74.9 %copy-start.10 = (f32[256]{0:T(256)S(1)}, f32[256]{0:T(256)}, u32[]{:S(2)}) copy-start(f32[256]{0:T(256)} %copy-done.8) | copy-start | bytes 3076
  502.0 41.4 %collective-permute-start.8 = (f32[512,2560]{1,0:T(8,128)}, f32[512,2560]{1,0:T(8,128)}, u32[]{:S(2)}, u32[]{:S(2)}) collective-permute-start(f32[512,2560]{1,0:T(8,128)} %get-tuple-element.83), channel_id=1, source_target_pairs={{0,1},{1,0},{2,3},{3,2},{4,5},{5,4},{6,7},{7,6},{8,9},{9,8},{10,11... | collective-permute-start | bytes 15728648 | tf_op jit(solution)/shard_map/ppermute | solution.py:658
Sparse Core Ops, SparseCore 0:
  223.4 203.8 all-gather.5
  429.5 87.1 all-gather.3

commit v3 on v2

--- a/solution.py
+++ b/solution.py
@@ -42,12 +42,13 @@
     ('r22,r51,r03,x2,s3,r13,f1,r23,r52,r04,s4,r31,r14,r24', 'r53,x3,r41,f2,r32,r54,x4,f3,r42,f4,r33,r43,r34,r44'),
 )
 VOCAB_BLOCK = 1280
-GRAD_CHUNKS = (208, 64)
-ROW_BLOCK = 512
+GRAD_CHUNKS = (216, 48)
+ROW_BLOCK = 528
 BLOCK_CALLS = (1, 1, 1, 1)
 TOKEN_BLOCK = 1024
 POS_BLOCK = 2
-OWN_POS_BLOCK = 4
+OWN_POS_BLOCK = 2
+OWN_DEPTH = 4
 PLACE_BLOCK = 4
 
 
@@ -355,8 +356,29 @@
             for arr in gathered]
 
 
-def own_rows_kernel(inv_n, bases, where, emb0_ref, emb1_ref, all_ref, all_stats_ref, own0_ref, own1_ref, emb_ref, acc_ref):
+def own_rows_kernel(inv_n, bases, where, emb0_ref, emb1_ref, all_ref, all_stats_ref, own0_ref, own1_ref,
+                    emb_ref, acc_ref, stage_ref, sem):
     n0, n1 = emb0_ref.shape[0], emb1_ref.shape[0]
+    step, n_steps = pl.program_id(0), pl.num_programs(0)
+    depth, n_pos = stage_ref.shape[0], stage_ref.shape[1]
+    per_core = all_ref.shape[1] // n_pos
+
+    def load(i):
+        src = all_ref.at[i // per_core, pl.ds(lax.rem(i, per_core) * n_pos, n_pos)]
+        slot = lax.rem(i, depth)
+        return pltpu.make_async_copy(src, stage_ref.at[slot], sem.at[slot])
+
+    @pl.when(step == 0)
+    def _():
+        for i in range(depth - 1):
+            load(i).start()
+
+    load(step).wait()
+
+    @pl.when(step + depth - 1 < n_steps)
+    def _():
+        load(step + depth - 1).start()
+
 
     @pl.when(pl.program_id(0) == 0)
     def _():
@@ -367,7 +389,7 @@
     first0, first1 = [where[1] + base + where[0] * n for base, n in zip(bases, (n0, n1))]
     row = lax.broadcasted_iota(jnp.int32, (n0 + n1, 1), 0)
     row_ids = (row + jnp.where(row < n0, first0, first1 - n0)).astype(jnp.float32)
-    h_blk, stats = load_tokens(all_ref, all_stats_ref)
+    h_blk, stats = load_tokens(stage_ref.at[pl.ds(lax.rem(step, depth), 1)], all_stats_ref)
     acc_ref[...] += row_grads(inv_n, emb_ref[...], row_ids, h_blk, stats)
 
     @pl.when(pl.program_id(0) == pl.num_programs(0) - 1)
@@ -390,9 +412,12 @@
         grid_spec=pltpu.PrefetchScalarGridSpec(
             num_scalar_prefetch=1,
             grid=(gathered[0].shape[0] * gathered[0].shape[1] // OWN_POS_BLOCK,),
-            in_specs=[emb_spec(bases[0], n0), emb_spec(bases[1], n1)] + token_specs(gathered, OWN_POS_BLOCK),
+            in_specs=[emb_spec(bases[0], n0), emb_spec(bases[1], n1),
+                      pl.BlockSpec(memory_space=pl.ANY), token_specs(gathered, OWN_POS_BLOCK)[1]],
             out_specs=(whole(n0), whole(n1 + 8)),
-            scratch_shapes=[pltpu.VMEM((n0 + n1, width), jnp.bfloat16), pltpu.VMEM((n0 + n1, width), jnp.float32)]),
+            scratch_shapes=[pltpu.VMEM((n0 + n1, width), jnp.bfloat16), pltpu.VMEM((n0 + n1, width), jnp.float32),
+                            pltpu.VMEM((OWN_DEPTH, OWN_POS_BLOCK) + gathered[0].shape[2:], jnp.float32),
+                            pltpu.SemaphoreType.DMA((OWN_DEPTH,))]),
         compiler_params=pltpu.CompilerParams(vmem_limit_bytes=VMEM_LIMIT),
         cost_estimate=pl.CostEstimate(
             flops=4 * (n0 + n1) * n_tok * width, bytes_accessed=n_tok * width * 4, transcendentals=(n0 + n1) * n_tok),
@@ -542,7 +567,7 @@
         args += [got, *recvs]
         in_specs += [anywhere] * (1 + len(recvs))
         part = ROW_BLOCK * len(recvs) // n_steps
-        part = next(n for n in range(max(part, 8), ROW_BLOCK + 1, 8) if ROW_BLOCK % n == 0 and n * n_steps >= ROW_BLOCK * len(recvs))
+        part = next(n for n in range(part // 8 * 8 or 8, ROW_BLOCK + 1, 8) if ROW_BLOCK % n == 0 and n * n_steps >= ROW_BLOCK * len(recvs))
         scratch = [pltpu.VMEM((2, got.shape[0] // n_steps, n_got, width), jnp.float32),
                    pltpu.VMEM((2, part, width), jnp.float32), pltpu.SemaphoreType.DMA((4, 2))]
     rows = n_blocks * ROW_BLOCK
@@ -565,29 +590,38 @@
     )(where, *args)
 
 
-def place_kernel(where, src_ref, prev_ref, dst_ref):
+def place_kernel(where, src_ref, prev_ref, dst_ref, *sum_refs):
     del where, prev_ref
     n_dev, n_rows = src_ref.shape[0], dst_ref.shape[0] // src_ref.shape[0]
     for i in range(n_dev):
         dst_ref[i * n_rows:(i + 1) * n_rows] = src_ref[i, :n_rows]
-
-
-def place_rows(src, n_rows, out, where, first_block, per_block):
+    for sum_ref in sum_refs:
+        @pl.when(pl.program_id(0) == 0)
+        def _(sum_ref=sum_ref):
+            sum_ref[...] = jnp.zeros_like(sum_ref)
+
+        sum_ref[...] += sum(src_ref[i, n_rows:] for i in range(n_dev))
+
+
+def place_rows(src, n_rows, out, where, first_block, per_block, with_sums=False):
     n_src, n_in, width = src.shape
-    return pl.pallas_call(
+    placed = pl.pallas_call(
         place_kernel,
-        out_shape=jax.ShapeDtypeStruct(out.shape, out.dtype),
+        out_shape=[jax.ShapeDtypeStruct(out.shape, out.dtype)]
+                  + [jax.ShapeDtypeStruct((n_in - n_rows, width), out.dtype)] * with_sums,
         grid_spec=pltpu.PrefetchScalarGridSpec(
             num_scalar_prefetch=1,
             grid=(n_src // per_block,),
             in_specs=[pl.BlockSpec((per_block, n_in, width), lambda i, where: (i, 0, 0)),
                       pl.BlockSpec(memory_space=pl.ANY)],
-            out_specs=pl.BlockSpec((per_block * n_rows, width), lambda i, where: (i + first_block + where[3], 0))),
+            out_specs=[pl.BlockSpec((per_block * n_rows, width), lambda i, where: (i + first_block + where[3], 0))]
+                      + [pl.BlockSpec((n_in - n_rows, width), lambda i, where: (0, 0))] * with_sums),
         input_output_aliases={2: 0},
         compiler_params=pltpu.CompilerParams(vmem_limit_bytes=VMEM_LIMIT),
         cost_estimate=pl.CostEstimate(flops=src.size * 80, bytes_accessed=src.size * 8, transcendentals=0),
         name="place_rows",
     )(where, src, out)
+    return placed if with_sums else placed[0]
 
 
 def shifts(n_tp):
@@ -672,10 +706,9 @@
             n_own = GRAD_CHUNKS[1]
             n_place = PLACE_BLOCK * n_own
             (recv, block), (last_recv, last_block) = late
-            out = place_rows(recv.reshape(-1, ROW_BLOCK, d_model), ROW_BLOCK, out, where, block, 1)
-            out = place_rows(got1, n_own, out, jnp.zeros_like(where), n_dp * GRAD_CHUNKS[0] // n_place, PLACE_BLOCK)
-            out = place_rows(last_recv.reshape(-1, ROW_BLOCK, d_model), ROW_BLOCK, out, where, last_block, 1)
-            sums = jnp.sum(got1[:, n_own:n_own + 2], axis=0)
+            for part, start in ((recv, block), (last_recv, last_block)):
+                out = place_rows(part.reshape(-1, ROW_BLOCK, d_model), ROW_BLOCK, out, where, start, 1)
+            out, sums = place_rows(got1, n_own, out, jnp.zeros_like(where), n_dp * GRAD_CHUNKS[0] // n_place, PLACE_BLOCK, True)
             return sums[1, 0], grad_r.reshape(n_batch, n_seq, d_model), out, sums[0]
 
         sharded = jax.shard_map(

time: 558 us -> 555 us (level)
  waiting for transfers between devices: 19.4 us -> 11.8 us
    all_gather x1, waiting for transfers between devices: 10.7 us -> 0.01 us  [local_part(): got1 = lax.all_gather(own1, 'dp')]
  transfers between devices with their start and end apart: 12 -> 12, of which waited for: 2 -> 1; matrix products, arithmetic and copies ran while one was open for 3% -> 2% of each run, Pallas kernels for 49% -> 48%
where the time goes in v3:
time: 555 us; the launch traced here: 552 us
  Pallas kernels  489 us (88%)
  between operations  15 us (3%)
  other arithmetic  14.4 us (3%)
  waiting for transfers between devices  11.8 us (2%)
  local copies, waits for them, and re-layouts  10.8 us (2%)
  starting transfers between devices  10.7 us (2%)
    pallas_call x3, Pallas kernels, grad_rows(): pl.pallas_call(functools.partial(grad_rows_kernel, inv_n, first, n_steps,...  189 us
    pallas_call x1, Pallas kernels, exchange_tokens(): pl.pallas_call(functools.partial(exchange_kernel, plan, PIECES, SHARE_ROW...  172 us
    pallas_call x1, Pallas kernels, first_block(): pl.pallas_call(functools.partial(first_block_kernel, inv_n, first), out_s...  65.5 us
    pallas_call x1, Pallas kernels, own_rows(): pl.pallas_call(functools.partial(own_rows_kernel, inv_n, bases), out_shap...  36.6 us
    pallas_call x3, Pallas kernels, place_rows(): pl.pallas_call(place_kernel, out_shape=[jax.ShapeDtypeStruct(out.shape, o...  26 us
    all_gather x1, waiting for transfers between devices, local_part(): got0 = lax.all_gather(own0, 'dp')  11.8 us
  transfers between devices with their start and end apart: 12, of which 1 were waited for; matrix products, arithmetic and copies ran while one was open for 2% of the time, Pallas kernels for 48%

profile of v3, /device:TPU:0, one launch (start us, length us, event | category | flops | bytes accessed | tf_op | source)
XLA Modules:
  0.0 552.2 jit_solution(17130935062022421803)
XLA Ops:
  7.2 1.3 fusion.7
  8.7 0.7 compare_select_fusion.ids_ref
  9.4 2.5 fusion.2
  11.9 2.7 fusion.5
  14.7 0.6 pad_add_fusion.where
  15.3 172.3 %exchange_tokens.1 = (f32[2,16,256,2560]{3,2,1,0:T(8,128)}, f32[2,16,8,512]{3,2,1,0:T(8,128)}, f32[256,2560]{1,0:T(8,128)}, f32[8,256]{1,0:T(8,128)}) custom-call(bf16[256,2560]{1,0:T(8,128)(2,1)} %get-tuple-element.92.h_ref, f32[256,2560]{1,0:T(8,128)} %get-tuple-element.93.own_ref, bf16[12572,2560]{1,0:T(8,128)(2,1)} %emb_ref.9, ...), custom_call_target="tpu_custom_call" | custom-call | flops 494351155200 | bytes 128737280 | tf_op jit(solution)/shard_map/exchange_tokens/pallas_call | solution.py:315
  187.6 36.6 %own_rows.1 = (f32[216,2560]{1,0:T(8,128)}, f32[56,2560]{1,0:T(8,128)}) custom-call(s32[4]{0:T(128)} %pad_add_fusion.where, bf16[12572,2560]{1,0:T(8,128)(2,1)} %emb_ref.9, bf16[12572,2560]{1,0:T(8,128)(2,1)} %emb_ref.9, f32[2,16,256,2560]{3,2,1,0:T(8,128)} %get-tuple-element.65.all_ref, f32[2,16,8,512]{3,2,1,0:T(8,128)} %get-tuple-element.66.all_stats_ref), custom_call_target="tpu_custom_call" | custom-call | flops 22145925120 | bytes 83886080 | tf_op jit(solution)/shard_map/own_rows/pallas_call | solution.py:409
  224.4 1.3 dynamic-slice_bitcast_fusion
  225.7 0.4 collective-permute-start
  226.2 2.0 collective-permute-start.1
  228.2 1.7 collective-permute-start.2
  229.9 65.5 %first_block.1 = (f32[12572,2560]{1,0:T(8,128)}, f32[528,2560]{1,0:T(8,128)}, bf16[8192,2560]{1,0:T(8,128)(2,1)}, f32[8,8192]{1,0:T(8,128)}) custom-call(s32[4]{0:T(128)} %pad_add_fusion.where, bf16[12572,2560]{1,0:T(8,128)(2,1)} %emb_ref.9, f32[2,16,256,2560]{3,2,1,0:T(8,128)} %get-tuple-element.65.all_ref, f32[2,16,8,512]{3,2,1,0:T(8,128)} %get-tuple-element.66.all_stats_ref), custom_call_target="tpu_custom_call" | custom-call | flops 44291850240 | bytes 125829120 | tf_op jit(solution)/shard_map/first_block/pallas_call | solution.py:452
  295.4 1.4 subtract_reduce_fusion
  298.0 1.9 collective-permute-start.4
  299.9 2.5 collective-permute-start.5
  302.4 56.0 %grad_rows.3 = (f32[12572,2560]{1,0:T(8,128)}, f32[528,2560]{1,0:T(8,128)}) custom-call(s32[4]{0:T(128)} %pad_add_fusion.where, bf16[12572,2560]{1,0:T(8,128)(2,1)} %emb_ref.9, bf16[8192,2560]{1,0:T(8,128)(2,1)} %get-tuple-element.72.h_ref, f32[8,8192]{1,0:T(8,128)} %get-tuple-element.73.stats_ref, ...), custom_call_target="tpu_custom_call", output_to_operand_aliasing={{0}: (4, {})} | custom-call | flops 44291850240 | bytes 50053120 | tf_op jit(solution)/shard_map/grad_rows/pallas_call | solution.py:574
  359.0 2.5 copy-done.1
  361.6 1.3 multiply_reduce_fusion
  362.8 1.6 scatter.6
  364.4 1.3 scatter.9
  365.8 0.5 collective-permute-start.7
  366.3 56.2 %grad_rows.4 = (f32[12572,2560]{1,0:T(8,128)}, f32[528,2560]{1,0:T(8,128)}) custom-call(s32[4]{0:T(128)} %pad_add_fusion.where, bf16[12572,2560]{1,0:T(8,128)(2,1)} %emb_ref.9, bf16[8192,2560]{1,0:T(8,128)(2,1)} %get-tuple-element.72.h_ref, f32[8,8192]{1,0:T(8,128)} %get-tuple-element.73.stats_ref, ...), custom_call_target="tpu_custom_call", output_to_operand_aliasing={{0}: (4, {})} | custom-call | flops 44291850240 | bytes 50053120 | tf_op jit(solution)/shard_map/grad_rows/pallas_call | solution.py:574
  422.5 1.0 collective-permute-start.9
  423.5 11.8 %all-gather.6.cloned.1.call-done = f32[6912,2560]{1,0:T(8,128)} async-done(((f32[216,2560]{1,0:T(8,128)}), f32[6912,2560]{1,0:T(8,128)}) %all-gather.6.cloned.1.call-update) | async-done | bytes 70778896 | tf_op jit(solution)/shard_map/all_gather | solution.py:676
  435.3 76.8 %grad_rows.5 = (f32[12572,2560]{1,0:T(8,128)}, f32[528,2560]{1,0:T(8,128)}) custom-call(s32[4]{0:T(128)} %pad_add_fusion.where, bf16[12572,2560]{1,0:T(8,128)(2,1)} %emb_ref.9, bf16[8192,2560]{1,0:T(8,128)(2,1)} %get-tuple-element.72.h_ref, f32[8,8192]{1,0:T(8,128)} %get-tuple-element.73.stats_ref, ...), custom_call_target="tpu_custom_call", output_to_operand_aliasing={{0}: (4, {})} | custom-call | flops 44291850240 | bytes 50053120 | tf_op jit(solution)/shard_map/grad_rows/pallas_call | solution.py:574
  512.3 3.8 fusion.1
  516.1 6.0 %place_rows.3.prev_ref = f32[12572,2560]{1,0:T(8,128)} custom-call(s32[4]{0:T(128)} %pad_add_fusion.where, f32[1,528,2560]{2,1,0:T(8,128)} %bitcast.20.src_ref, f32[12572,2560]{1,0:T(8,128)} %get-tuple-element.87.prev_ref), custom_call_target="tpu_custom_call", output_to_operand_aliasing={{}: (2, {})} | custom-call | flops 108134400 | bytes 10813440 | tf_op jit(solution)/shard_map/place_rows/pallas_call | solution.py:608
  522.0 5.6 %place_rows.4.prev_ref = f32[12572,2560]{1,0:T(8,128)} custom-call(s32[4]{0:T(128)} %pad_add_fusion.where, f32[1,528,2560]{2,1,0:T(8,128)} %bitcast.19.src_ref, f32[12572,2560]{1,0:T(8,128)} %place_rows.3.prev_ref), custom_call_target="tpu_custom_call", output_to_operand_aliasing={{}: (2, {})} | custom-call | flops 108134400 | bytes 10813440 | tf_op jit(solution)/shard_map/place_rows/pallas_call | solution.py:608
  527.7 0.5 broadcast_2_where.2.where
  528.2 14.4 %place_rows.5 = (f32[12572,2560]{1,0:T(8,128)}, f32[8,2560]{1,0:T(8,128)}) custom-call(s32[4]{0:T(128)} %broadcast_2_where.2.where, f32[32,56,2560]{2,1,0:T(8,128)} %all-gather.4.cloned.1.call-done.src_ref, f32[12572,2560]{1,0:T(8,128)} %place_rows.4.prev_ref), custom_call_target="tpu_custom_call", output_to_operand_aliasing={{0}: (2, {})} | custom-call | flops 367001600 | bytes 36700160 | tf_op jit(solution)/shard_map/place_rows/pallas_call | solution.py:608
  542.6 1.5 slice_reduce_fusion
  544.1 1.2 slice.52
  (53 shorter events, 1.8 us)
Async XLA Ops:
  7.2 428.1 %all-gather.6.cloned.1.call-start = ((), (), s32[]{:S(2)}) async-start(), calls=%async_computation.1 | async-start | bytes 72990720 | tf_op jit(solution)/shard_map/all_gather | solution.py:676
  9.4 2.6 copy-start.5
  11.9 2.8 copy-start
  11.9 2.8 copy-start.8
  187.6 36.8 %copy-start.4 = (f32[256,2560]{1,0:T(8,128)S(1)}, f32[256,2560]{1,0:T(8,128)}, u32[]{:S(2)}) copy-start(f32[256,2560]{1,0:T(8,128)} %get-tuple-element.64) | copy-start | bytes 7864324
  224.3 303.4 %all-gather.4.cloned.1.call-start = ((), (), s32[]{:S(2)}) async-start(), calls=%async_computation | async-start | bytes 18923520 | tf_op jit(solution)/shard_map/all_gather | solution.py:704
  225.7 71.8 %collective-permute-start = (f32[64,2560]{1,0:T(8,128)}, f32[64,2560]{1,0:T(8,128)S(1)}, u32[]{:S(2)}, u32[]{:S(2)}) collective-permute-start(f32[64,2560]{1,0:T(8,128)} %get-tuple-element.98), channel_id=1, source_target_pairs={{0,32},{32,64},{64,96},{96,0},{1,33},{33,65},{65,97},{97,1},{2,34}... | collective-permute-start | bytes 1966088 | tf_op jit(solution)/shard_map/ppermute | solution.py:634
  226.2 71.4 %collective-permute-start.1 = (f32[64,2560]{1,0:T(8,128)}, f32[64,2560]{1,0:T(8,128)S(1)}, u32[]{:S(2)}, u32[]{:S(2)}) collective-permute-start(f32[64,2560]{1,0:T(8,128)} %get-tuple-element.97), channel_id=1, source_target_pairs={{0,64},{32,96},{64,0},{96,32},{1,65},{33,97},{65,1},{97,33},{2,66}... | collective-permute-start | bytes 1966088 | tf_op jit(solution)/shard_map/ppermute | solution.py:634
  228.2 67.2 %copy-start.9 = (f32[256]{0:T(256)S(1)}, f32[256]{0:T(256)}, u32[]{:S(2)}) copy-start(f32[256]{0:T(256)} %copy-done.8) | copy-start | bytes 3076
  228.2 69.3 %collective-permute-start.2 = (f32[64,2560]{1,0:T(8,128)}, f32[64,2560]{1,0:T(8,128)S(1)}, u32[]{:S(2)}, u32[]{:S(2)}) collective-permute-start(f32[64,2560]{1,0:T(8,128)} %get-tuple-element.96), channel_id=1, source_target_pairs={{0,96},{32,0},{64,32},{96,64},{1,97},{33,1},{65,33},{97,65},{2,98}... | collective-permute-start | bytes 1966088 | tf_op jit(solution)/shard_map/ppermute | solution.py:634
  297.7 60.8 %collective-permute-start.3 = (f32[64,2560]{1,0:T(8,128)S(1)}, f32[64,2560]{1,0:T(8,128)S(1)}, u32[]{:S(2)}, u32[]{:S(2)}) collective-permute-start(f32[64,2560]{1,0:T(8,128)S(1)} %add_add_fusion), channel_id=1, source_target_pairs={{0,32},{32,64},{64,96},{96,0},{1,33},{33,65},{65,97},{97,1},{2,34}... | collective-permute-start | bytes 1966088 | tf_op jit(solution)/shard_map/ppermute | solution.py:639
  298.0 60.4 %collective-permute-start.4 = (f32[64,2560]{1,0:T(8,128)S(1)}, f32[64,2560]{1,0:T(8,128)S(1)}, u32[]{:S(2)}, u32[]{:S(2)}) collective-permute-start(f32[64,2560]{1,0:T(8,128)S(1)} %add_add_fusion), channel_id=1, source_target_pairs={{0,64},{32,96},{64,0},{96,32},{1,65},{33,97},{65,1},{97,33},{2,66}... | collective-permute-start | bytes 1966088 | tf_op jit(solution)/shard_map/ppermute | solution.py:639
  299.9 58.6 %collective-permute-start.5 = (f32[64,2560]{1,0:T(8,128)S(1)}, f32[64,2560]{1,0:T(8,128)S(1)}, u32[]{:S(2)}, u32[]{:S(2)}) collective-permute-start(f32[64,2560]{1,0:T(8,128)S(1)} %add_add_fusion), channel_id=1, source_target_pairs={{0,96},{32,0},{64,32},{96,64},{1,97},{33,1},{65,33},{97,65},{2,98}... | collective-permute-start | bytes 1966088 | tf_op jit(solution)/shard_map/ppermute | solution.py:639
  358.8 2.8 copy-start.1
  358.8 2.8 copy-start.6
  359.0 3.8 copy-start.3
  365.7 57.9 %collective-permute-start.6 = (f32[528,2560]{1,0:T(8,128)}, f32[528,2560]{1,0:T(8,128)}, u32[]{:S(2)}, u32[]{:S(2)}) collective-permute-start(f32[528,2560]{1,0:T(8,128)} %get-tuple-element.83), channel_id=1, source_target_pairs={{0,1},{1,0},{2,3},{3,2},{4,5},{5,4},{6,7},{7,6},{8,9},{9,8},{10,11... | collective-permute-start | bytes 16220168 | tf_op jit(solution)/shard_map/ppermute | solution.py:692
  365.8 57.8 %collective-permute-start.7 = (f32[528,2560]{1,0:T(8,128)}, f32[528,2560]{1,0:T(8,128)}, u32[]{:S(2)}, u32[]{:S(2)}) collective-permute-start(f32[528,2560]{1,0:T(8,128)} %get-tuple-element.84), channel_id=1, source_target_pairs={{0,1},{1,0},{2,3},{3,2},{4,5},{5,4},{6,7},{7,6},{8,9},{9,8},{10,11... | collective-permute-start | bytes 16220168 | tf_op jit(solution)/shard_map/ppermute | solution.py:692
  422.5 93.6 %collective-permute-start.9 = (f32[528,2560]{1,0:T(8,128)}, f32[528,2560]{1,0:T(8,128)}, u32[]{:S(2)}, u32[]{:S(2)}) collective-permute-start(f32[528,2560]{1,0:T(8,128)} %get-tuple-element.86), channel_id=1, source_target_pairs={{0,1},{1,0},{2,3},{3,2},{4,5},{5,4},{6,7},{7,6},{8,9},{9,8},{10,11... | collective-permute-start | bytes 16220168 | tf_op jit(solution)/shard_map/ppermute | solution.py:692
  435.3 76.9 %copy-start.11 = (f32[4,64]{1,0:T(4,128)S(1)}, f32[4,64]{1,0:T(4,128)}, u32[]{:S(2)}) copy-start(f32[4,64]{1,0:T(4,128)} %get-tuple-element.90) | copy-start | bytes 3076
  435.3 77.0 %copy-start.2 = (f32[1,256,2560]{2,1,0:T(8,128)S(1)}, f32[1,256,2560]{2,1,0:T(8,128)}, u32[]{:S(2)}) copy-start(f32[1,256,2560]{2,1,0:T(8,128)} %copy-done) | copy-start | bytes 7864324
  435.3 77.0 %copy-start.7 = (f32[2560]{0:T(1024)S(1)}, f32[2560]{0:T(1024)}, u32[]{:S(2)}) copy-start(f32[2560]{0:T(1024)} %param.13) | copy-start | bytes 30724
  435.3 77.0 %copy-start.10 = (f32[256]{0:T(256)S(1)}, f32[256]{0:T(256)}, u32[]{:S(2)}) copy-start(f32[256]{0:T(256)} %copy-done.8) | copy-start | bytes 3076
  512.1 10.0 %collective-permute-start.8 = (f32[528,2560]{1,0:T(8,128)}, f32[528,2560]{1,0:T(8,128)}, u32[]{:S(2)}, u32[]{:S(2)}) collective-permute-start(f32[528,2560]{1,0:T(8,128)} %get-tuple-element.85), channel_id=1, source_target_pairs={{0,1},{1,0},{2,3},{3,2},{4,5},{5,4},{6,7},{7,6},{8,9},{9,8},{10,11... | collective-permute-start | bytes 16220168 | tf_op jit(solution)/shard_map/ppermute | solution.py:692
Sparse Core Ops, SparseCore 0:
  224.4 210.8 all-gather.5
  437.6 72.6 all-gather.3

commit v4 on v3

--- a/solution.py
+++ b/solution.py
@@ -42,9 +42,9 @@
     ('r22,r51,r03,x2,s3,r13,f1,r23,r52,r04,s4,r31,r14,r24', 'r53,x3,r41,f2,r32,r54,x4,f3,r42,f4,r33,r43,r34,r44'),
 )
 VOCAB_BLOCK = 1280
-GRAD_CHUNKS = (216, 48)
-ROW_BLOCK = 528
-BLOCK_CALLS = (1, 1, 1, 1)
+GRAD_CHUNKS = (192, 64)
+ROW_BLOCK = 576
+BLOCK_CALLS = (2, 1, 1)
 TOKEN_BLOCK = 1024
 POS_BLOCK = 2
 OWN_POS_BLOCK = 2
@@ -143,15 +143,18 @@
     def wait(self, ref, sem):
         pltpu.make_async_copy(ref, ref, sem).wait()
 
-    def finish_round(self, p, piece, k):
-        n, rows = len(HOPS[k]), self.rows(piece)
-        self.wait(self.whole(piece).at[0, pl.ds(0, n), pl.ds(0, piece[2])], self.sems['plane_recv'].at[p, k - 1])
+    def wait_round(self, p, piece, k):
+        blocks = self.whole(piece).at[0, pl.ds(0, len(HOPS[k])), pl.ds(0, piece[2])]
+        self.wait(blocks, self.sems['plane_recv'].at[p, k - 1])
+
+    def forward(self, piece, k):
+        rows = self.rows(piece)
         for hop in HOPS[k]:
             ref = self.block(piece, hop, rows)
-            self.to_pair(piece, ref, ref)
             if piece[0] == 'share':
                 for s in (1, -1):
                     self.send(ref, ref, self.at(dx=s), 'x_send', self.sems['x_recv'].at[k - 1])
+            self.to_pair(piece, ref, ref)
 
     def share_of(self, dx):
         x = lax.rem(self.x + dx + RING, RING)
@@ -201,9 +204,10 @@
             ex.round(nums[0], pieces[nums[0]], 1)
         elif kind == 'r':
             p, k = nums
-            ex.finish_round(p, pieces[p], k)
+            ex.wait_round(p, pieces[p], k)
             if k < 4:
                 ex.round(p, pieces[p], k + 1)
+            ex.forward(pieces[p], k)
         elif kind == 'x':
             ex.along_x(nums[0])
         else:
@@ -216,9 +220,10 @@
             def _(i=i, events=events):
                 if i == 0:
                     ex.barrier()
-                    ex.start_own(pieces[0])
                 for event in events:
                     run(event)
+                if i == 0:
+                    ex.start_own(pieces[0])
                 if i == len(plan) - 1:
                     ex.finish(pieces)
 
@@ -333,8 +338,11 @@
     )(h_act, h_wide, emb, local_ids, tgt_row)
 
 
-def row_grads(inv_n, emb, row_ids, h_blk, stats):
-    logits = lax.dot_general(emb, h_blk, NT, preferred_element_type=jnp.float32)
+def row_grads(inv_n, emb, row_ids, h_blk, stats, few_rows=False):
+    if few_rows:
+        logits = lax.dot_general(h_blk, emb, NT, preferred_element_type=jnp.float32).T
+    else:
+        logits = lax.dot_general(emb, h_blk, NT, preferred_element_type=jnp.float32)
     prob = jnp.exp(logits - stats[0:1]) * stats[1:2]
     grad = prob - jnp.where(row_ids == stats[2:3], inv_n, 0.0)
     return jnp.dot(grad.astype(jnp.bfloat16), h_blk, preferred_element_type=jnp.float32)
@@ -390,7 +398,7 @@
     row = lax.broadcasted_iota(jnp.int32, (n0 + n1, 1), 0)
     row_ids = (row + jnp.where(row < n0, first0, first1 - n0)).astype(jnp.float32)
     h_blk, stats = load_tokens(stage_ref.at[pl.ds(lax.rem(step, depth), 1)], all_stats_ref)
-    acc_ref[...] += row_grads(inv_n, emb_ref[...], row_ids, h_blk, stats)
+    acc_ref[...] += row_grads(inv_n, emb_ref[...], row_ids, h_blk, stats, True)
 
     @pl.when(pl.program_id(0) == pl.num_programs(0) - 1)
     def _():
@@ -436,7 +444,7 @@
     h_ref[...] = h_blk
     stats_ref[...] = stats
     n_rows = emb_ref.shape[0]
-    row_ids = id_column(n_rows, where[1] + (where[2] + first) * n_rows)
+    row_ids = id_column(n_rows, where[1] + where[2] * ROW_BLOCK + first)
     out_ref[...] += row_grads(inv_n, emb_ref[...], row_ids, h_blk, stats)
 
     @pl.when(step == last)
@@ -444,27 +452,28 @@
         copy_ref[...] = out_ref[...]
 
 
-def first_block(emb, gathered, where, inv_n, first):
+def first_block(emb, gathered, where, inv_n, first, n_blocks):
     vocab, width = emb.shape
     n_tok = gathered[0].size // width
     per_step = POS_BLOCK * gathered[0].shape[2]
-    row_spec = pl.BlockSpec((ROW_BLOCK, width), lambda i, where: (first + where[2], 0))
+    rows = n_blocks * ROW_BLOCK
+    row_spec = pl.BlockSpec((rows, width), lambda i, where: ((first + where[2]) // n_blocks, 0), pipeline_mode=pl.Buffered(1))
     return pl.pallas_call(
-        functools.partial(first_block_kernel, inv_n, first),
+        functools.partial(first_block_kernel, inv_n, first * ROW_BLOCK),
         out_shape=(jax.ShapeDtypeStruct((vocab, width), jnp.float32),
-                   jax.ShapeDtypeStruct((ROW_BLOCK, width), jnp.float32),
+                   jax.ShapeDtypeStruct((rows, width), jnp.float32),
                    jax.ShapeDtypeStruct((n_tok, width), jnp.bfloat16),
                    jax.ShapeDtypeStruct((8, n_tok), jnp.float32)),
         grid_spec=pltpu.PrefetchScalarGridSpec(
             num_scalar_prefetch=1,
             grid=(n_tok // per_step,),
             in_specs=[row_spec] + token_specs(gathered, POS_BLOCK),
-            out_specs=(row_spec, pl.BlockSpec((ROW_BLOCK, width), lambda i, where: (0, 0)),
+            out_specs=(row_spec, pl.BlockSpec((rows, width), lambda i, where: (0, 0), pipeline_mode=pl.Buffered(1)),
                        pl.BlockSpec((per_step, width), lambda i, where: (i, 0)),
                        pl.BlockSpec((8, per_step), lambda i, where: (0, i)))),
         compiler_params=pltpu.CompilerParams(vmem_limit_bytes=VMEM_LIMIT),
         cost_estimate=pl.CostEstimate(
-            flops=4 * ROW_BLOCK * n_tok * width, bytes_accessed=n_tok * width * 6, transcendentals=ROW_BLOCK * n_tok),
+            flops=4 * rows * n_tok * width, bytes_accessed=n_tok * width * 6, transcendentals=rows * n_tok),
         name="first_block",
     )(where, emb, *gathered)
 
@@ -528,7 +537,7 @@
 
 
 def grad_rows_kernel(inv_n, first, n_steps, recv_firsts, where, emb_ref, h_ref, stats_ref, *refs):
-    i, t = pl.program_id(0), pl.program_id(1)
+    step = pl.program_id(0)
     n_ref = 2 + len(recv_firsts) if recv_firsts else 1
     out_in_ref, acc_ref, copy_ref = refs[0], refs[n_ref], refs[n_ref + 1]
     n_rows = emb_ref.shape[0]
@@ -536,56 +545,54 @@
     if recv_firsts:
         rows = [(where[3] + block) * n_rows for block in recv_firsts]
         placing = Placing(out_in_ref, refs[1], refs[2:n_ref], rows, n_steps, refs[n_ref + 2:n_ref + 4], refs[n_ref + 4])
-        placing.before(i * pl.num_programs(1) + t)
-
-    @pl.when(t == 0)
+        placing.before(step)
+
+    @pl.when(step == 0)
     def _():
         acc_ref[...] = jnp.zeros_like(acc_ref)
 
-    row_ids = id_column(n_rows, where[1] + (where[2] + first + i) * n_rows)
+    row_ids = id_column(n_rows, where[1] + (where[2] + first) * n_rows)
     acc_ref[...] += row_grads(inv_n, emb_ref[...], row_ids, h_ref[...], stats_ref[...])
 
-    @pl.when(t == pl.num_programs(1) - 1)
+    @pl.when(step == pl.num_programs(0) - 1)
     def _():
         copy_ref[...] = acc_ref[...]
 
     if placing:
-        placing.after(i * pl.num_programs(1) + t)
-
-
-def grad_rows(emb, h_all, stats, where, out, inv_n, first, n_blocks, got=None, n_got=0, recvs=(), recv_firsts=()):
+        placing.after(step)
+
+
+def grad_rows(emb, h_all, stats, where, out, inv_n, first, got=None, n_got=0, recvs=(), recv_firsts=()):
     vocab, width = emb.shape
     n_tok = h_all.shape[0]
     tok_block = min(TOKEN_BLOCK, n_tok)
-    n_steps = n_blocks * (n_tok // tok_block)
-    row_spec = pl.BlockSpec((ROW_BLOCK, width), lambda i, t, where: (i + first + where[2], 0))
+    n_steps = n_tok // tok_block
+    row_spec = pl.BlockSpec((ROW_BLOCK, width), lambda t, where: (first + where[2], 0), pipeline_mode=pl.Buffered(1))
     anywhere = pl.BlockSpec(memory_space=pl.ANY)
-    in_specs = [row_spec, pl.BlockSpec((tok_block, width), lambda i, t, where: (t, 0)),
-                pl.BlockSpec((8, tok_block), lambda i, t, where: (0, t)), anywhere]
+    in_specs = [row_spec, pl.BlockSpec((tok_block, width), lambda t, where: (t, 0)),
+                pl.BlockSpec((8, tok_block), lambda t, where: (0, t)), anywhere]
     args, scratch = [emb, h_all, stats, out], []
     if recvs:
         args += [got, *recvs]
         in_specs += [anywhere] * (1 + len(recvs))
-        part = ROW_BLOCK * len(recvs) // n_steps
-        part = next(n for n in range(part // 8 * 8 or 8, ROW_BLOCK + 1, 8) if ROW_BLOCK % n == 0 and n * n_steps >= ROW_BLOCK * len(recvs))
+        n_recv = recvs[0].shape[0]
+        part = n_recv * len(recvs) // n_steps
+        part = next(n for n in range(part // 8 * 8 or 8, n_recv + 1, 8) if n_recv % n == 0 and n * n_steps >= n_recv * len(recvs))
         scratch = [pltpu.VMEM((2, got.shape[0] // n_steps, n_got, width), jnp.float32),
                    pltpu.VMEM((2, part, width), jnp.float32), pltpu.SemaphoreType.DMA((4, 2))]
-    rows = n_blocks * ROW_BLOCK
     return pl.pallas_call(
         functools.partial(grad_rows_kernel, inv_n, first, n_steps, tuple(recv_firsts)),
-        out_shape=(jax.ShapeDtypeStruct((vocab, width), jnp.float32), jax.ShapeDtypeStruct((rows, width), jnp.float32)),
+        out_shape=(jax.ShapeDtypeStruct((vocab, width), jnp.float32), jax.ShapeDtypeStruct((ROW_BLOCK, width), jnp.float32)),
         grid_spec=pltpu.PrefetchScalarGridSpec(
             num_scalar_prefetch=1,
-            grid=(n_blocks, n_tok // tok_block),
+            grid=(n_steps,),
             in_specs=in_specs,
-            out_specs=(row_spec, pl.BlockSpec((ROW_BLOCK, width), lambda i, t, where: (i, 0))),
+            out_specs=(row_spec, pl.BlockSpec((ROW_BLOCK, width), lambda t, where: (0, 0), pipeline_mode=pl.Buffered(1))),
             scratch_shapes=scratch),
         input_output_aliases={4: 0},
         compiler_params=pltpu.CompilerParams(vmem_limit_bytes=VMEM_LIMIT),
         cost_estimate=pl.CostEstimate(
-            flops=4 * rows * n_tok * width,
-            bytes_accessed=rows * width * 6 + n_blocks * n_tok * width * 2,
-            transcendentals=rows * n_tok),
+            flops=4 * ROW_BLOCK * n_tok * width, bytes_accessed=n_tok * width * 2, transcendentals=ROW_BLOCK * n_tok),
         name="grad_rows",
     )(where, *args)
 
@@ -679,13 +686,13 @@
 
             first = n_dp * sum(GRAD_CHUNKS) // ROW_BLOCK
             pair = [(i, i ^ 1) for i in range(n_dp)]
-            out, copied, h_all, all_stats = first_block(emb_loc, gathered, where, inv_n, first)
+            out, copied, h_all, all_stats = first_block(emb_loc, gathered, where, inv_n, first, BLOCK_CALLS[0])
             recvs, recv_firsts, late, block = [], [], [], first
             for c, n_blocks in enumerate(BLOCK_CALLS):
                 final = c == len(BLOCK_CALLS) - 1
                 if c:
                     extra = (got0, GRAD_CHUNKS[0], recvs, recv_firsts) if final else ()
-                    out, copied = grad_rows(emb_loc, h_all, all_stats, where, out, inv_n, block, n_blocks, *extra)
+                    out, copied = grad_rows(emb_loc, h_all, all_stats, where, out, inv_n, block, *extra)
                 if c < 2:
                     grad_h, out = lax.optimization_barrier((grad_h, out))
                     grad_h = join_totals(grad_h, n_tp, tp_idx) if c else send_total(grad_h, n_tp)

time: 555 us -> 586 us (1.056)
  Pallas kernels: 489 us -> 516 us
  waiting for transfers between devices: 11.8 us -> 17.9 us
    pallas_call x1, Pallas kernels: 65.5 us -> 123 us  [first_block(): pl.pallas_call(functools.partial(first_block_kernel, inv_n, first * ROW_B...]
    pallas_call x3 -> x2, Pallas kernels: 189 us -> 135 us  [grad_rows(): pl.pallas_call(functools.partial(grad_rows_kernel, inv_n, first, n_steps,...]
    pallas_call x1, Pallas kernels: 36.6 us -> 55.4 us  [own_rows(): pl.pallas_call(functools.partial(own_rows_kernel, inv_n, bases), out_shap...]
    ppermute x4 -> x3, waiting for transfers between devices: 0.01 us -> 17.9 us  [local_part(): recv = lax.ppermute(copied, 'dp', pair)]
    all_gather x1, waiting for transfers between devices: 11.8 us -> 0.01 us  [local_part(): got0 = lax.all_gather(own0, 'dp')]
  transfers between devices with their start and end apart: 12 -> 11, of which waited for: 1 -> 1; matrix products, arithmetic and copies ran while one was open for 2% -> 2% of each run, Pallas kernels for 48% -> 46%
where the time goes in v4:
time: 586 us; the launch traced here: 584 us
  Pallas kernels  516 us (88%)
  waiting for transfers between devices  17.9 us (3%)
  between operations  15 us (3%)
  other arithmetic  13.8 us (2%)
  local copies, waits for them, and re-layouts  11.5 us (2%)
  starting transfers between devices  9.44 us (2%)
    pallas_call x1, Pallas kernels, exchange_tokens(): pl.pallas_call(functools.partial(exchange_kernel, plan, PIECES, SHARE_ROW...  173 us
    pallas_call x2, Pallas kernels, grad_rows(): pl.pallas_call(functools.partial(grad_rows_kernel, inv_n, first, n_steps,...  135 us
    pallas_call x1, Pallas kernels, first_block(): pl.pallas_call(functools.partial(first_block_kernel, inv_n, first * ROW_B...  123 us
    pallas_call x1, Pallas kernels, own_rows(): pl.pallas_call(functools.partial(own_rows_kernel, inv_n, bases), out_shap...  55.4 us
    pallas_call x3, Pallas kernels, place_rows(): pl.pallas_call(place_kernel, out_shape=[jax.ShapeDtypeStruct(out.shape, o...  29.5 us
    ppermute x3, waiting for transfers between devices, local_part(): recv = lax.ppermute(copied, 'dp', pair)  17.9 us
  transfers between devices with their start and end apart: 11, of which 1 were waited for; matrix products, arithmetic and copies ran while one was open for 2% of the time, Pallas kernels for 46%

profile of v4, /device:TPU:0, one launch (start us, length us, event | category | flops | bytes accessed | tf_op | source)
XLA Modules:
  0.0 583.8 jit_solution(10353240035210606230)
XLA Ops:
  7.2 1.3 fusion.7
  8.7 0.7 compare_select_fusion.ids_ref
  9.4 2.5 fusion.2
  11.9 2.7 fusion.5
  14.7 0.6 pad_add_fusion.where
  15.3 172.5 %exchange_tokens.1 = (f32[2,16,256,2560]{3,2,1,0:T(8,128)}, f32[2,16,8,512]{3,2,1,0:T(8,128)}, f32[256,2560]{1,0:T(8,128)}, f32[8,256]{1,0:T(8,128)}) custom-call(bf16[256,2560]{1,0:T(8,128)(2,1)} %get-tuple-element.88.h_ref, f32[256,2560]{1,0:T(8,128)} %get-tuple-element.89.own_ref, bf16[12572,2560]{1,0:T(8,128)(2,1)} %emb_ref.7, ...), custom_call_target="tpu_custom_call" | custom-call | flops 494351155200 | bytes 128737280 | tf_op jit(solution)/shard_map/exchange_tokens/pallas_call | solution.py:320
  187.9 55.4 %own_rows.1 = (f32[192,2560]{1,0:T(8,128)}, f32[72,2560]{1,0:T(8,128)}) custom-call(s32[4]{0:T(128)} %pad_add_fusion.where, bf16[12572,2560]{1,0:T(8,128)(2,1)} %emb_ref.7, bf16[12572,2560]{1,0:T(8,128)(2,1)} %emb_ref.7, f32[2,16,256,2560]{3,2,1,0:T(8,128)} %get-tuple-element.63.all_ref, f32[2,16,8,512]{3,2,1,0:T(8,128)} %get-tuple-element.64.all_stats_ref), custom_call_target="tpu_custom_call" | custom-call | flops 21474836480 | bytes 83886080 | tf_op jit(solution)/shard_map/own_rows/pallas_call | solution.py:417
  243.5 1.4 dynamic-slice_bitcast_fusion
  244.8 0.4 collective-permute-start
  245.2 2.0 collective-permute-start.1
  247.3 1.7 collective-permute-start.2
  249.0 123.3 %first_block.1 = (f32[12572,2560]{1,0:T(8,128)}, f32[1152,2560]{1,0:T(8,128)}, bf16[8192,2560]{1,0:T(8,128)(2,1)}, f32[8,8192]{1,0:T(8,128)}) custom-call(s32[4]{0:T(128)} %pad_add_fusion.where, bf16[12572,2560]{1,0:T(8,128)(2,1)} %emb_ref.7, f32[2,16,256,2560]{3,2,1,0:T(8,128)} %get-tuple-element.63.all_ref, f32[2,16,8,512]{3,2,1,0:T(8,128)} %get-tuple-element.64.all_stats_ref), custom_call_target="tpu_custom_call" | custom-call | flops 96636764160 | bytes 125829120 | tf_op jit(solution)/shard_map/first_block/pallas_call | solution.py:461
  372.3 1.4 subtract_reduce_fusion
  374.8 1.8 collective-permute-start.4
  376.6 2.5 collective-permute-start.5
  379.1 60.3 %grad_rows.2 = (f32[12572,2560]{1,0:T(8,128)}, f32[576,2560]{1,0:T(8,128)}) custom-call(s32[4]{0:T(128)} %pad_add_fusion.where, bf16[12572,2560]{1,0:T(8,128)(2,1)} %emb_ref.7, bf16[8192,2560]{1,0:T(8,128)(2,1)} %get-tuple-element.70.h_ref, f32[8,8192]{1,0:T(8,128)} %get-tuple-element.71.stats_ref, ...), custom_call_target="tpu_custom_call", output_to_operand_aliasing={{0}: (4, {})} | custom-call | flops 48318382080 | bytes 41943040 | tf_op jit(solution)/shard_map/grad_rows/pallas_call | solution.py:583
  439.5 0.8 copy-done.6
  441.0 1.3 bitcast_dynamic-update-slice_fusion.1
  442.4 0.7 copy-done.1
  443.1 0.7 multiply_reduce_fusion
  443.9 1.6 scatter.6
  445.4 1.3 scatter.9
  446.8 0.5 collective-permute-start.8
  447.3 17.9 %collective-permute-done.6.refs_2_ = f32[1152,2560]{1,0:T(8,128)} collective-permute-done((f32[1152,2560]{1,0:T(8,128)}, f32[1152,2560]{1,0:T(8,128)}, u32[]{:S(2)}, u32[]{:S(2)}) %collective-permute-start.6) | collective-permute-done | bytes 11796512 | tf_op jit(solution)/shard_map/ppermute | solution.py:699
  465.2 75.0 %grad_rows.3 = (f32[12572,2560]{1,0:T(8,128)}, f32[576,2560]{1,0:T(8,128)}) custom-call(s32[4]{0:T(128)} %pad_add_fusion.where, bf16[12572,2560]{1,0:T(8,128)(2,1)} %emb_ref.7, bf16[8192,2560]{1,0:T(8,128)(2,1)} %get-tuple-element.70.h_ref, f32[8,8192]{1,0:T(8,128)} %get-tuple-element.71.stats_ref, ...), custom_call_target="tpu_custom_call", output_to_operand_aliasing={{0}: (4, {})} | custom-call | flops 48318382080 | bytes 41943040 | tf_op jit(solution)/shard_map/grad_rows/pallas_call | solution.py:583
  540.4 3.8 fusion.1
  544.2 6.3 %place_rows.3.prev_ref = f32[12572,2560]{1,0:T(8,128)} custom-call(s32[4]{0:T(128)} %pad_add_fusion.where, f32[1,576,2560]{2,1,0:T(8,128)} %bitcast.20.src_ref, f32[12572,2560]{1,0:T(8,128)} %get-tuple-element.83.prev_ref), custom_call_target="tpu_custom_call", output_to_operand_aliasing={{}: (2, {})} | custom-call | flops 117964800 | bytes 11796480 | tf_op jit(solution)/shard_map/place_rows/pallas_call | solution.py:615
  550.5 6.0 %place_rows.4.prev_ref = f32[12572,2560]{1,0:T(8,128)} custom-call(s32[4]{0:T(128)} %pad_add_fusion.where, f32[1,576,2560]{2,1,0:T(8,128)} %bitcast.19.src_ref, f32[12572,2560]{1,0:T(8,128)} %place_rows.3.prev_ref), custom_call_target="tpu_custom_call", output_to_operand_aliasing={{}: (2, {})} | custom-call | flops 117964800 | bytes 11796480 | tf_op jit(solution)/shard_map/place_rows/pallas_call | solution.py:615
  556.5 0.5 broadcast_2_where.2.where
  557.0 17.3 %place_rows.5 = (f32[12572,2560]{1,0:T(8,128)}, f32[8,2560]{1,0:T(8,128)}) custom-call(s32[4]{0:T(128)} %broadcast_2_where.2.where, f32[32,72,2560]{2,1,0:T(8,128)} %all-gather.4.cloned.1.call-done.src_ref, f32[12572,2560]{1,0:T(8,128)} %place_rows.4.prev_ref), custom_call_target="tpu_custom_call", output_to_operand_aliasing={{0}: (2, {})} | custom-call | flops 471859200 | bytes 47185920 | tf_op jit(solution)/shard_map/place_rows/pallas_call | solution.py:615
  574.3 1.5 slice_reduce_fusion
  575.8 1.2 slice.52
  (54 shorter events, 2.0 us)
Async XLA Ops:
  7.2 458.0 %all-gather.6.cloned.1.call-start = ((), (), s32[]{:S(2)}) async-start(), calls=%async_computation.1 | async-start | bytes 64880640 | tf_op jit(solution)/shard_map/all_gather | solution.py:683
  9.4 2.6 copy-start.9
  11.9 2.8 copy-start
  11.9 2.8 copy-start.11
  187.9 55.6 %copy-start.3 = (f32[256,2560]{1,0:T(8,128)S(1)}, f32[256,2560]{1,0:T(8,128)}, u32[]{:S(2)}) copy-start(f32[256,2560]{1,0:T(8,128)} %get-tuple-element.62) | copy-start | bytes 7864324
  243.3 313.1 %all-gather.4.cloned.1.call-start = ((), (), s32[]{:S(2)}) async-start(), calls=%async_computation | async-start | bytes 24330240 | tf_op jit(solution)/shard_map/all_gather | solution.py:711
  244.8 129.6 %collective-permute-start = (f32[64,2560]{1,0:T(8,128)}, f32[64,2560]{1,0:T(8,128)S(1)}, u32[]{:S(2)}, u32[]{:S(2)}) collective-permute-start(f32[64,2560]{1,0:T(8,128)} %get-tuple-element.94), channel_id=1, source_target_pairs={{0,32},{32,64},{64,96},{96,0},{1,33},{33,65},{65,97},{97,1},{2,34}... | collective-permute-start | bytes 1966088 | tf_op jit(solution)/shard_map/ppermute | solution.py:641
  245.2 129.1 %collective-permute-start.1 = (f32[64,2560]{1,0:T(8,128)}, f32[64,2560]{1,0:T(8,128)S(1)}, u32[]{:S(2)}, u32[]{:S(2)}) collective-permute-start(f32[64,2560]{1,0:T(8,128)} %get-tuple-element.93), channel_id=1, source_target_pairs={{0,64},{32,96},{64,0},{96,32},{1,65},{33,97},{65,1},{97,33},{2,66}... | collective-permute-start | bytes 1966088 | tf_op jit(solution)/shard_map/ppermute | solution.py:641
  247.3 124.9 %copy-start.12 = (f32[256]{0:T(256)S(1)}, f32[256]{0:T(256)}, u32[]{:S(2)}) copy-start(f32[256]{0:T(256)} %copy-done.11) | copy-start | bytes 3076
  247.3 127.1 %collective-permute-start.2 = (f32[64,2560]{1,0:T(8,128)}, f32[64,2560]{1,0:T(8,128)S(1)}, u32[]{:S(2)}, u32[]{:S(2)}) collective-permute-start(f32[64,2560]{1,0:T(8,128)} %get-tuple-element.92), channel_id=1, source_target_pairs={{0,96},{32,0},{64,32},{96,64},{1,97},{33,1},{65,33},{97,65},{2,98}... | collective-permute-start | bytes 1966088 | tf_op jit(solution)/shard_map/ppermute | solution.py:641
  374.5 64.9 %copy-start.4 = (f32[64,2560]{1,0:T(8,128)}, f32[64,2560]{1,0:T(8,128)S(1)}, u32[]{:S(2)}) copy-start(f32[64,2560]{1,0:T(8,128)S(1)} %add_add_fusion) | copy-start | bytes 1966084
  374.6 64.9 %collective-permute-start.3 = (f32[64,2560]{1,0:T(8,128)S(1)}, f32[64,2560]{1,0:T(8,128)S(1)}, u32[]{:S(2)}, u32[]{:S(2)}) collective-permute-start(f32[64,2560]{1,0:T(8,128)S(1)} %add_add_fusion), channel_id=1, source_target_pairs={{0,32},{32,64},{64,96},{96,0},{1,33},{33,65},{65,97},{97,1},{2,34}... | collective-permute-start | bytes 1966088 | tf_op jit(solution)/shard_map/ppermute | solution.py:646
  374.8 64.7 %collective-permute-start.4 = (f32[64,2560]{1,0:T(8,128)S(1)}, f32[64,2560]{1,0:T(8,128)S(1)}, u32[]{:S(2)}, u32[]{:S(2)}) collective-permute-start(f32[64,2560]{1,0:T(8,128)S(1)} %add_add_fusion), channel_id=1, source_target_pairs={{0,64},{32,96},{64,0},{96,32},{1,65},{33,97},{65,1},{97,33},{2,66}... | collective-permute-start | bytes 1966088 | tf_op jit(solution)/shard_map/ppermute | solution.py:646
  376.6 62.9 %collective-permute-start.5 = (f32[64,2560]{1,0:T(8,128)S(1)}, f32[64,2560]{1,0:T(8,128)S(1)}, u32[]{:S(2)}, u32[]{:S(2)}) collective-permute-start(f32[64,2560]{1,0:T(8,128)S(1)} %add_add_fusion), channel_id=1, source_target_pairs={{0,96},{32,0},{64,32},{96,64},{1,97},{33,1},{65,33},{97,65},{2,98}... | collective-permute-start | bytes 1966088 | tf_op jit(solution)/shard_map/ppermute | solution.py:646
  439.4 1.5 copy-start.5
  439.4 0.9 copy-start.6
  439.5 1.0 copy-start.7
  440.9 1.4 copy-start.8
  440.9 2.1 copy-start.1
  440.9 2.1 copy-start.10
  442.4 1.5 copy-start.2
  446.7 18.5 %collective-permute-start.6 = (f32[1152,2560]{1,0:T(8,128)}, f32[1152,2560]{1,0:T(8,128)}, u32[]{:S(2)}, u32[]{:S(2)}) collective-permute-start(f32[1152,2560]{1,0:T(8,128)} %get-tuple-element.80), channel_id=1, source_target_pairs={{0,1},{1,0},{2,3},{3,2},{4,5},{5,4},{6,7},{7,6},{8,9},{9,8},{10,11... | collective-permute-start | bytes 35389448 | tf_op jit(solution)/shard_map/ppermute | solution.py:699
  446.8 97.4 %collective-permute-start.8 = (f32[576,2560]{1,0:T(8,128)}, f32[576,2560]{1,0:T(8,128)}, u32[]{:S(2)}, u32[]{:S(2)}) collective-permute-start(f32[576,2560]{1,0:T(8,128)} %get-tuple-element.82), channel_id=1, source_target_pairs={{0,1},{1,0},{2,3},{3,2},{4,5},{5,4},{6,7},{7,6},{8,9},{9,8},{10,11... | collective-permute-start | bytes 17694728 | tf_op jit(solution)/shard_map/ppermute | solution.py:699
  465.2 75.2 %copy-start.13 = (f32[256]{0:T(256)S(1)}, f32[256]{0:T(256)}, u32[]{:S(2)}) copy-start(f32[256]{0:T(256)} %copy-done.11) | copy-start | bytes 3076
  540.2 10.3 %collective-permute-start.7 = (f32[576,2560]{1,0:T(8,128)}, f32[576,2560]{1,0:T(8,128)}, u32[]{:S(2)}, u32[]{:S(2)}) collective-permute-start(f32[576,2560]{1,0:T(8,128)} %get-tuple-element.81), channel_id=1, source_target_pairs={{0,1},{1,0},{2,3},{3,2},{4,5},{5,4},{6,7},{7,6},{8,9},{9,8},{10,11... | collective-permute-start | bytes 17694728 | tf_op jit(solution)/shard_map/ppermute | solution.py:699
Sparse Core Ops, SparseCore 0:
  243.5 187.2 all-gather.5
  446.9 84.9 all-gather.3
